TPU v7x, 32 devices: a whole 2x2x4 slice. The times are simulated.
32 devices in a mesh: seq: 16 (over z, y, core), batch: 2 (over x).
Axes of the slice: x: 2, y: 2, z: 4, core: 2. Of those that a mesh axis runs over, the one named last changes fastest.
Arguments:
- queries: bfloat16 [4096, 1792], P(('batch', 'seq')), parts along dimension 0, may hold values from -128 to 128
- keys: bfloat16 [4096, 256], P(('batch', 'seq')), parts along dimension 0, may hold values from -4 to 4
- values: bfloat16 [4096, 256], P(('batch', 'seq')), parts along dimension 0, may hold values from -4 to 4
- out_grad: bfloat16 [4096, 1792], P(('batch', 'seq')), parts along dimension 0, may hold values from -24 to 24
- row_delta: float32 [4096, 14], P(('batch', 'seq')), parts along dimension 0, may hold values from -6 to 6
- layer_input: bfloat16 [4096, 3584], P(('batch', 'seq')), parts along dimension 0, may hold values from -6 to 6
- norm_gain: float32 [3584], replicated, may hold values from 0.25 to 1.75
- qkv_weight: bfloat16 [3584, 2304], P('seq'), may hold values from -0.5 to 0.5
- block_order: int32 [64], P('batch'), parts along dimension 0, may hold values from 0 to 31, as said below
- block_mask: int32 [64, 32], P('batch'), parts along dimension 0, may hold values from 0 to 1, as said below
- frame_owner: int32 [32], P('batch'), parts along dimension 0, may hold values from 0 to 15, as said below
- vision_features: bfloat16 [32, 128, 1152], P(('batch', 'seq')), parts along dimension 0, may hold values from -6 to 6
- post_gain: float32 [1152], replicated, may hold values from 0.25 to 1.75
- projector: bfloat16 [1152, 3584], replicated, may hold values from -0.1875 to 0.1875
Outputs:
- token_grad: bfloat16 [4096, 3584], P(('batch', 'seq')), parts along dimension 0
- encoder_grad: bfloat16 [32, 128, 1152], P(('batch', 'seq')), parts along dimension 0
There are 2 independent parts, one for each index of `batch`. A program takes and returns all parts, laid end to end along the dimension named above; an argument that names none is the same for every part. Nothing has to cross between parts.
Inputs may be any that keep to these rules, and one draw needn't show every extreme that they name: `block_order`: entries 2i and 2i + 1 are the blocks of device i of seq; all entries together are a permutation; each device's two blocks sum to 31; for every frame f, blocks 2f and 2f + 1 lie on devices 2j and 2j + 1 for some j. `block_mask`: 1 on the diagonal, 0 above it. `frame_owner`: every device of seq owns exactly one frame, and the owner of frame f holds block 2f or block 2f + 1.
All inputs are finite; a program needn't handle non-finite values.
Results may differ from a plain program's by a relative error of at most 0.012.
Values may be sent and summed in bfloat16 or wider, within the bound.
A program may use at most 128 MiB of HBM per device.

v0:
```python
import jax
import jax.numpy as jnp
from jax import lax
from jax.sharding import PartitionSpec as P

HQ = 14
KVH = 2
HD = 128


EPSILON = 1e-06
NEGATIVE = -1e30


def shifted(value, axis, steps):
    count = lax.axis_size(axis)
    pairs = [(source, (source + steps) % count) for source in range(count)]
    return lax.ppermute(value, axis, pairs)


def for_sending(array):
    return jax.tree.map(lambda a: a.astype(jnp.bfloat16) if a.dtype == jnp.float32 else a, array)


def swapped(array, axis, apart):
    return lax.ppermute(array, axis, [(i, i ^ 1 << apart) for i in range(lax.axis_size(axis))])


def pick_blocks(block_order, slot_ids):
    table = jnp.arange(block_order.shape[0], dtype=jnp.int32)
    matched = slot_ids[:, None] == table[None, :]
    return jnp.sum(jnp.where(matched, block_order[None, :], 0), axis=1)


def key_mask(query_pos, query_live, block_order, first_row, key_rows, half_len):
    row_ids = first_row + jnp.arange(key_rows, dtype=jnp.int32)
    key_blocks = pick_blocks(block_order, row_ids // half_len)
    key_pos = key_blocks * half_len + row_ids % half_len
    table = jnp.arange(block_order.shape[0], dtype=jnp.int32)
    key_onehot = (key_blocks[:, None] == table[None, :]).astype(jnp.int32)
    allowed = jnp.dot(query_live, key_onehot.T)
    return (allowed > 0) & (key_pos[None, :] <= query_pos[:, None])


def score_block(query_part, keys_here, scaling):
    return (
        jnp.einsum("qkgd,tkd->kgqt", query_part, keys_here, preferred_element_type=jnp.float32)
        * scaling
    )


def block_grads(
    query_part, grad_part, lse_part, delta_part, keys_here, values_here, allowed, scaling
):
    score = score_block(query_part, keys_here, scaling)
    prob = jnp.where(allowed, jnp.exp(score - lse_part[..., None]), 0.0)
    prob_low = prob.astype(jnp.bfloat16)
    value_add = jnp.einsum(
        "kgqt,qkgd->tkd", prob_low, grad_part, preferred_element_type=jnp.float32
    )
    prob_grad = jnp.einsum(
        "qkgd,tkd->kgqt", grad_part, values_here, preferred_element_type=jnp.float32
    )
    score_grad = (prob * (prob_grad - delta_part[..., None])).astype(jnp.bfloat16)
    query_add = jnp.einsum(
        "kgqt,tkd->qkgd", score_grad, keys_here, preferred_element_type=jnp.float32
    )
    key_add = jnp.einsum(
        "kgqt,qkgd->tkd", score_grad, query_part, preferred_element_type=jnp.float32
    )
    return (query_add, key_add, value_add)


def body(
    queries,
    keys,
    values,
    out_grad,
    row_delta,
    layer_input,
    norm_gain,
    qkv_weight,
    block_order,
    block_mask,
    frame_owner,
    vision_features,
    post_gain,
    projector,
):
    tok_rows = queries.shape[0]
    half_len = tok_rows // 2
    cycle_size = lax.axis_size("seq")
    my_index = lax.axis_index("seq")
    group_size = HQ // KVH
    scaling = HD ** (-0.5)
    block_count = block_order.shape[0]
    block_table = jnp.arange(block_count, dtype=jnp.int32)
    my_blocks = lax.dynamic_slice_in_dim(block_order, 2 * my_index, 2, 0)
    query_pos = (
        my_blocks[:, None] * half_len + jnp.arange(half_len, dtype=jnp.int32)[None, :]
    ).reshape(tok_rows)
    my_onehot = (my_blocks[:, None] == block_table[None, :]).astype(jnp.int32)
    query_live = jnp.repeat(jnp.dot(my_onehot, block_mask), half_len, axis=0)
    query_five = queries.reshape(tok_rows, KVH, group_size, HD)
    grad_five = out_grad.reshape(tok_rows, KVH, group_size, HD)
    key_three = keys.reshape(tok_rows, KVH, HD)
    value_three = values.reshape(tok_rows, KVH, HD)
    delta_rows = jnp.transpose(row_delta.reshape(tok_rows, KVH, group_size), (1, 2, 0))
    zero_stats = (
        jnp.full((KVH, group_size, tok_rows), NEGATIVE, jnp.float32),
        jnp.zeros((KVH, group_size, tok_rows), jnp.float32),
    )
    key_piece = lax.all_gather(keys, "seq", axis=0, tiled=True)
    shards = key_piece.shape[0] // tok_rows
    stacked = key_piece.reshape(shards, tok_rows, KVH, HD)

    def absorb(current, shard_entry):
        top_now, total_now = current
        keys_here, shard_index = shard_entry
        allowed = key_mask(
            query_pos, query_live, block_order, shard_index * tok_rows, tok_rows, half_len
        )
        score = score_block(query_five, keys_here, scaling)
        top_next = jnp.maximum(top_now, jnp.max(jnp.where(allowed, score, NEGATIVE), axis=-1))
        spread = jnp.where(allowed, jnp.exp(score - top_next[..., None]), 0.0)
        return (
            (top_next, total_now * jnp.exp(top_now - top_next) + jnp.sum(spread, axis=-1)),
            None,
        )

    result, unused = lax.scan(absorb, zero_stats, (stacked, jnp.arange(shards, dtype=jnp.int32)))
    lse_rows = result[0] + jnp.log(result[1])

    def absorb_source(kv_pair, kv_grads, source):
        allowed = key_mask(
            query_pos, query_live, block_order, source * tok_rows, tok_rows, half_len
        )
        query_add, key_add, value_add = block_grads(
            query_five, grad_five, lse_rows, delta_rows, kv_pair[0], kv_pair[1], allowed, scaling
        )
        return (query_add, (kv_grads[0] + key_add, kv_grads[1] + value_add))

    query_acc = jnp.zeros((tok_rows, KVH, group_size, HD), jnp.float32)

    def pass_grads(kv_grads):
        return shifted(kv_grads, "seq", 1)

    def cycle_turn(step_index, running):
        kv_pair, kv_grads, query_sum = running
        source = (my_index - step_index) % cycle_size
        query_add, kv_grads = absorb_source(kv_pair, kv_grads, source)
        kv_pair = jax.tree.map(
            lambda part, own: part.astype(own.dtype),
            shifted(for_sending(kv_pair), "seq", 1),
            kv_pair,
        )
        return (kv_pair, pass_grads(kv_grads), query_sum + query_add)

    zero_grads = (
        jnp.zeros((tok_rows, KVH, HD), jnp.float32),
        jnp.zeros((tok_rows, KVH, HD), jnp.float32),
    )
    kv_pair, kv_grads, query_acc = lax.fori_loop(
        0, cycle_size - 1, cycle_turn, ((key_three, value_three), zero_grads, query_acc)
    )
    query_add, kv_grads = absorb_source(kv_pair, kv_grads, (my_index + 1) % cycle_size)
    key_sum, value_sum = pass_grads(kv_grads)
    query_acc = query_acc + query_add
    query_grad = (query_acc * scaling).astype(jnp.bfloat16).reshape(tok_rows, HQ * HD)
    key_grad = (key_sum * scaling).astype(jnp.bfloat16).reshape(tok_rows, KVH * HD)
    value_grad = value_sum.astype(jnp.bfloat16).reshape(tok_rows, KVH * HD)
    head_grads = jnp.concatenate([query_grad, key_grad, value_grad], axis=1)
    norm_grad = jnp.dot(
        head_grads,
        lax.all_gather(qkv_weight, "seq", axis=0, tiled=True).T,
        preferred_element_type=jnp.float32,
    ).astype(jnp.bfloat16)
    inputs = layer_input.astype(jnp.float32)
    inverse = lax.rsqrt(jnp.mean(inputs * inputs, axis=1, keepdims=True) + EPSILON)
    scaled = norm_grad.astype(jnp.float32) * norm_gain
    token_grad = (
        inverse * scaled - inputs * inverse**3 * jnp.mean(scaled * inputs, axis=1, keepdims=True)
    ).astype(jnp.bfloat16)
    frame_table = jnp.arange(frame_owner.shape[0], dtype=jnp.int32)
    my_frame = jnp.sum(jnp.where(frame_owner == my_index, frame_table, 0))
    keep_first = my_blocks[0] // 2 == my_frame
    kept_block = jnp.where(keep_first, my_blocks[0], my_blocks[1])
    leading = kept_block % 2 == 0
    halves = token_grad.reshape(2, half_len, token_grad.shape[1])
    kept = jnp.where(keep_first, halves[0], halves[1])
    sending = jnp.where(keep_first, halves[1], halves[0])
    received = swapped(sending, "seq", 0)
    frame_rows = jnp.where(
        leading,
        jnp.concatenate([kept, received], axis=0),
        jnp.concatenate([received, kept], axis=0),
    )
    post_grad = jnp.dot(frame_rows, projector.T, preferred_element_type=jnp.float32)
    features = vision_features[0].astype(jnp.float32)
    centered = features - jnp.mean(features, axis=1, keepdims=True)
    deviation = lax.rsqrt(jnp.mean(centered * centered, axis=1, keepdims=True) + EPSILON)
    normed = centered * deviation
    weighted = post_grad * post_gain
    encoder_grad = (
        deviation
        * (
            weighted
            - jnp.mean(weighted, axis=1, keepdims=True)
            - normed * jnp.mean(weighted * normed, axis=1, keepdims=True)
        )
    ).astype(jnp.bfloat16)
    return (token_grad, encoder_grad[None])


def solution(mesh):
    placed = (
        P(("batch", "seq"), None),
        P(("batch", "seq"), None),
        P(("batch", "seq"), None),
        P(("batch", "seq"), None),
        P(("batch", "seq"), None),
        P(("batch", "seq"), None),
        P(),
        P("seq", None),
        P("batch"),
        P("batch", None),
        P("batch"),
        P(("batch", "seq"), None, None),
        P(),
        P(),
    )
    return jax.shard_map(
        body,
        mesh=mesh,
        in_specs=placed,
        out_specs=(P(("batch", "seq"), None), P(("batch", "seq"), None, None)),
        check_vma=False,
    )
```

profile of v0, /device:TPU:0, one launch (start us, length us, event | category | flops | bytes accessed | tf_op | source)
XLA Modules:
  0.0 392.9 jit_solution(1651288233358045467)
XLA Ops:
  22.0 28.8 %all-gather.3.cloned.1.call-done = bf16[2048,256]{1,0:T(8,128)(2,1)} async-done(((bf16[128,256]{1,0:T(8,128)(2,1)}), bf16[2048,256]{1,0:T(8,128)(2,1)}) %all-gather.3.cloned.1.call-update) | async-done | bytes 1048592 | tf_op jit(solution)/shard_map/all_gather | solution.py:113
  50.8 2.1 reshape.248
  52.9 84.4 %while.40 = (s32[]{:T(128)}, f32[2,7,128]{2,1,0:T(8,128)S(1)}, f32[2,7,128]{2,1,0:T(8,128)S(1)}, s32[16]{0:T(128)S(1)}, s32[32]{0:T(128)}, /*index=5*/bf16[16,12...) while((s32[]{:T(128)}, f32[2,7,128]{2,1,0:T(8,128)S(1)}, ...), condition=%wide.region_5.6_spmd.clone, body=%wide.region_1.5_spmd.clone.sunk | while | flops 61223424 | bytes 2671660 | solution.py:131
  138.0 216.4 %while.41 = (s32[]{:T(128)}, bf16[128,2,128]{2,0,1:T(8,128)(2,1)S(1)}, bf16[128,2,128]{2,0,1:T(8,128)(2,1)S(1)}, f32[128,2,128]{2,0,1:T(8,128)S(1)}, f32[128,2,1...) while((s32[]{:T(128)}, ...), condition=%wide.region_8.9_spmd.clone, body=%wide.region_6.8_spmd.clone.sunk | while | flops 296849152 | bytes 10441068 | solution.py:163
  144.1 1.4 collective-permute-start.3
  146.0 2.1 collective-permute-done.1
  148.1 5.5 %collective-permute-done.2 = f32[128,2,128]{2,0,1:T(8,128)S(1)} collective-permute-done((f32[128,2,128]{2,0,1:T(8,128)S(1)}, f32[128,2,128]{2,0,1:T(8,128)S(1)}, u32[]{:S(2)}, u32[]{:S(2)}) %collective-permute-start.2) | collective-permute-done | bytes 131104 | tf_op jit(solution)/shard_map/while/body/eval_jaxpr/ppermute | solution.py:18
  153.6 3.0 collective-permute-done.3
  162.9 1.7 collective-permute-done
  164.6 2.1 collective-permute-done.1
  166.7 5.0 %collective-permute-done.2 = f32[128,2,128]{2,0,1:T(8,128)S(1)} collective-permute-done((f32[128,2,128]{2,0,1:T(8,128)S(1)}, f32[128,2,128]{2,0,1:T(8,128)S(1)}, u32[]{:S(2)}, u32[]{:S(2)}) %collective-permute-start.2) | collective-permute-done | bytes 131104 | tf_op jit(solution)/shard_map/while/body/eval_jaxpr/ppermute | solution.py:18
  171.7 4.2 %collective-permute-done.3 = f32[128,2,128]{2,0,1:T(8,128)S(1)} collective-permute-done((f32[128,2,128]{2,0,1:T(8,128)S(1)}, f32[128,2,128]{2,0,1:T(8,128)S(1)}, u32[]{:S(2)}, u32[]{:S(2)}) %collective-permute-start.3) | collective-permute-done | bytes 131104 | tf_op jit(solution)/shard_map/while/body/eval_jaxpr/ppermute | solution.py:18
  183.9 4.1 %collective-permute-done.2 = f32[128,2,128]{2,0,1:T(8,128)S(1)} collective-permute-done((f32[128,2,128]{2,0,1:T(8,128)S(1)}, f32[128,2,128]{2,0,1:T(8,128)S(1)}, u32[]{:S(2)}, u32[]{:S(2)}) %collective-permute-start.2) | collective-permute-done | bytes 131104 | tf_op jit(solution)/shard_map/while/body/eval_jaxpr/ppermute | solution.py:18
  195.1 3.4 collective-permute-start.3
  198.9 2.6 collective-permute-done.2
  210.2 3.4 collective-permute-start.3
  214.1 1.8 collective-permute-done.2
  217.4 1.7 collective-permute-start.1
  225.9 5.3 %collective-permute-done.2 = f32[128,2,128]{2,0,1:T(8,128)S(1)} collective-permute-done((f32[128,2,128]{2,0,1:T(8,128)S(1)}, f32[128,2,128]{2,0,1:T(8,128)S(1)}, u32[]{:S(2)}, u32[]{:S(2)}) %collective-permute-start.2) | collective-permute-done | bytes 131104 | tf_op jit(solution)/shard_map/while/body/eval_jaxpr/ppermute | solution.py:18
  239.6 5.0 %collective-permute-done.2 = f32[128,2,128]{2,0,1:T(8,128)S(1)} collective-permute-done((f32[128,2,128]{2,0,1:T(8,128)S(1)}, f32[128,2,128]{2,0,1:T(8,128)S(1)}, u32[]{:S(2)}, u32[]{:S(2)}) %collective-permute-start.2) | collective-permute-done | bytes 131104 | tf_op jit(solution)/shard_map/while/body/eval_jaxpr/ppermute | solution.py:18
  253.2 5.0 %collective-permute-done.2 = f32[128,2,128]{2,0,1:T(8,128)S(1)} collective-permute-done((f32[128,2,128]{2,0,1:T(8,128)S(1)}, f32[128,2,128]{2,0,1:T(8,128)S(1)}, u32[]{:S(2)}, u32[]{:S(2)}) %collective-permute-start.2) | collective-permute-done | bytes 131104 | tf_op jit(solution)/shard_map/while/body/eval_jaxpr/ppermute | solution.py:18
  266.7 5.0 %collective-permute-done.2 = f32[128,2,128]{2,0,1:T(8,128)S(1)} collective-permute-done((f32[128,2,128]{2,0,1:T(8,128)S(1)}, f32[128,2,128]{2,0,1:T(8,128)S(1)}, u32[]{:S(2)}, u32[]{:S(2)}) %collective-permute-start.2) | collective-permute-done | bytes 131104 | tf_op jit(solution)/shard_map/while/body/eval_jaxpr/ppermute | solution.py:18
  280.2 5.0 %collective-permute-done.2 = f32[128,2,128]{2,0,1:T(8,128)S(1)} collective-permute-done((f32[128,2,128]{2,0,1:T(8,128)S(1)}, f32[128,2,128]{2,0,1:T(8,128)S(1)}, u32[]{:S(2)}, u32[]{:S(2)}) %collective-permute-start.2) | collective-permute-done | bytes 131104 | tf_op jit(solution)/shard_map/while/body/eval_jaxpr/ppermute | solution.py:18
  293.8 5.0 %collective-permute-done.2 = f32[128,2,128]{2,0,1:T(8,128)S(1)} collective-permute-done((f32[128,2,128]{2,0,1:T(8,128)S(1)}, f32[128,2,128]{2,0,1:T(8,128)S(1)}, u32[]{:S(2)}, u32[]{:S(2)}) %collective-permute-start.2) | collective-permute-done | bytes 131104 | tf_op jit(solution)/shard_map/while/body/eval_jaxpr/ppermute | solution.py:18
  307.3 5.0 %collective-permute-done.2 = f32[128,2,128]{2,0,1:T(8,128)S(1)} collective-permute-done((f32[128,2,128]{2,0,1:T(8,128)S(1)}, f32[128,2,128]{2,0,1:T(8,128)S(1)}, u32[]{:S(2)}, u32[]{:S(2)}) %collective-permute-start.2) | collective-permute-done | bytes 131104 | tf_op jit(solution)/shard_map/while/body/eval_jaxpr/ppermute | solution.py:18
  320.8 5.0 %collective-permute-done.2 = f32[128,2,128]{2,0,1:T(8,128)S(1)} collective-permute-done((f32[128,2,128]{2,0,1:T(8,128)S(1)}, f32[128,2,128]{2,0,1:T(8,128)S(1)}, u32[]{:S(2)}, u32[]{:S(2)}) %collective-permute-start.2) | collective-permute-done | bytes 131104 | tf_op jit(solution)/shard_map/while/body/eval_jaxpr/ppermute | solution.py:18
  334.4 5.0 %collective-permute-done.2 = f32[128,2,128]{2,0,1:T(8,128)S(1)} collective-permute-done((f32[128,2,128]{2,0,1:T(8,128)S(1)}, f32[128,2,128]{2,0,1:T(8,128)S(1)}, u32[]{:S(2)}, u32[]{:S(2)}) %collective-permute-start.2) | collective-permute-done | bytes 131104 | tf_op jit(solution)/shard_map/while/body/eval_jaxpr/ppermute | solution.py:18
  347.9 5.0 %collective-permute-done.2 = f32[128,2,128]{2,0,1:T(8,128)S(1)} collective-permute-done((f32[128,2,128]{2,0,1:T(8,128)S(1)}, f32[128,2,128]{2,0,1:T(8,128)S(1)}, u32[]{:S(2)}, u32[]{:S(2)}) %collective-permute-start.2) | collective-permute-done | bytes 131104 | tf_op jit(solution)/shard_map/while/body/eval_jaxpr/ppermute | solution.py:18
  359.1 6.6 %collective-permute-done.5 = bf16[128,2,128]{2,0,1:T(8,128)(2,1)S(1)} collective-permute-done((bf16[128,2,128]{2,0,1:T(8,128)(2,1)S(1)}, bf16[128,2,128]{2,0,1:T(8,128)(2,1)S(1)}, u32[]{:S(2)}, u32[]{:S(2)}) %collective-permute-start.5) | collective-permute-done | bytes 65568 | tf_op jit(solution)/shard_map/ppermute | solution.py:18
  366.1 9.2 %fusion.34 = (f32[128]{0:T(128)S(1)}, f32[128]{0:T(128)S(1)}, f32[128,3584]{1,0:T(8,128)S(1)}) fusion(bf16[128,3584]{1,0:T(8,128)(2,1)S(1)} %copy-done.5, f32[3584]{0:T(1024)S(1)} %copy-done.12, bf16[3584,2304]{1,0:T(8,128)(2,1)} %all-gather.5.cloned.1.call-done, bf16[128,256]{0,1:T(8,128)(2,1)S(1)} %bitcast.233, bf16[128,256]{0,1:T(8,128)(2,1)S(1)} %bitcast.234, ...), kind=kOutput, calls=%fused_computation.69 | convolution fusion | flops 2119368448 | bytes 19872768 | tf_op jit(solution)/shard_map/dot_general | solution.py:173
  375.3 1.6 fusion.37
  378.9 6.1 %fusion.87 = (f32[128]{0:T(128)S(1)}, f32[128]{0:T(128)S(1)}, f32[128,1152]{1,0:T(8,128)S(1)}) fusion(f32[128]{0:T(128)S(1)} %add_rsqrt_fusion, f32[128]{0:T(128)S(1)} %broadcast_multiply_fusion.2, bf16[1,128,1152]{2,1,0:T(8,128)(2,1)S(1)} %copy-done.7, f32[1152]{0:T(1024)S(1)} %copy-done.15, bf16[1152,3584]{1,0:T(8,128)(2,1)} %param.31, ...), kind=kOutput, calls=%fused_computation.154 | convolution fusion | flops 1062125312 | bytes 10066433 | tf_op jit(solution)/shard_map/dot_general | solution.py:198
  (620 shorter events, 214.1 us)
Async XLA Ops:
  7.2 43.6 %all-gather.3.cloned.1.call-start = ((), (), s32[]{:S(2)}) async-start(), calls=%async_computation | async-start | bytes 1114112 | tf_op jit(solution)/shard_map/all_gather | solution.py:113
  7.9 358.1 %all-gather.5.cloned.1.call-start = ((), (), s32[]{:S(2)}) async-start(), calls=%async_computation.1 | async-start | bytes 17547264 | tf_op jit(solution)/shard_map/all_gather | solution.py:175
  138.0 8.0 %collective-permute-start = (bf16[128,2,128]{2,0,1:T(8,128)(2,1)S(1)}, bf16[128,2,128]{2,0,1:T(8,128)(2,1)S(1)}, u32[]{:S(2)}, u32[]{:S(2)}) collective-permute-start(bf16[128,2,128]{2,0,1:T(8,128)(2,1)S(1)} %copy.108), channel_id=1, source_target_pairs={{0,2},{2,4},{4,6},{6,8},{8,10},{10,12},{12,14},{14,16},{16,18},{18... | collective-permute-start | bytes 196616 | tf_op jit(solution)/shard_map/while/body/eval_jaxpr/ppermute | solution.py:18
  138.3 9.8 %collective-permute-start.1 = (bf16[128,2,128]{2,0,1:T(8,128)(2,1)S(1)}, bf16[128,2,128]{2,0,1:T(8,128)(2,1)S(1)}, u32[]{:S(2)}, u32[]{:S(2)}) collective-permute-start(bf16[128,2,128]{2,0,1:T(8,128)(2,1)S(1)} %copy.109), channel_id=1, source_target_pairs={{0,2},{2,4},{4,6},{6,8},{8,10},{10,12},{12,14},{14,16},{16,18},{18... | collective-permute-start | bytes 196616 | tf_op jit(solution)/shard_map/while/body/eval_jaxpr/ppermute | solution.py:18
  143.5 10.1 %collective-permute-start.2 = (f32[128,2,128]{2,0,1:T(8,128)S(1)}, f32[128,2,128]{2,0,1:T(8,128)S(1)}, u32[]{:S(2)}, u32[]{:S(2)}) collective-permute-start(f32[128,2,128]{2,0,1:T(8,128)S(1)} %fusion.151), channel_id=1, source_target_pairs={{0,2},{2,4},{4,6},{6,8},{8,10},{10,12},{12,14},{14,16},{16,18},{18... | collective-permute-start | bytes 393224 | tf_op jit(solution)/shard_map/while/body/eval_jaxpr/ppermute | solution.py:18
  144.1 12.6 %collective-permute-start.3 = (f32[128,2,128]{2,0,1:T(8,128)S(1)}, f32[128,2,128]{2,0,1:T(8,128)S(1)}, u32[]{:S(2)}, u32[]{:S(2)}) collective-permute-start(f32[128,2,128]{2,0,1:T(8,128)S(1)} %fusion.152), channel_id=1, source_target_pairs={{0,2},{2,4},{4,6},{6,8},{8,10},{10,12},{12,14},{14,16},{16,18},{18... | collective-permute-start | bytes 393224 | tf_op jit(solution)/shard_map/while/body/eval_jaxpr/ppermute | solution.py:18
  156.6 7.9 %collective-permute-start = (bf16[128,2,128]{2,0,1:T(8,128)(2,1)S(1)}, bf16[128,2,128]{2,0,1:T(8,128)(2,1)S(1)}, u32[]{:S(2)}, u32[]{:S(2)}) collective-permute-start(bf16[128,2,128]{2,0,1:T(8,128)(2,1)S(1)} %copy.108), channel_id=1, source_target_pairs={{0,2},{2,4},{4,6},{6,8},{8,10},{10,12},{12,14},{14,16},{16,18},{18... | collective-permute-start | bytes 196616 | tf_op jit(solution)/shard_map/while/body/eval_jaxpr/ppermute | solution.py:18
  156.7 10.0 %collective-permute-start.1 = (bf16[128,2,128]{2,0,1:T(8,128)(2,1)S(1)}, bf16[128,2,128]{2,0,1:T(8,128)(2,1)S(1)}, u32[]{:S(2)}, u32[]{:S(2)}) collective-permute-start(bf16[128,2,128]{2,0,1:T(8,128)(2,1)S(1)} %copy.109), channel_id=1, source_target_pairs={{0,2},{2,4},{4,6},{6,8},{8,10},{10,12},{12,14},{14,16},{16,18},{18... | collective-permute-start | bytes 196616 | tf_op jit(solution)/shard_map/while/body/eval_jaxpr/ppermute | solution.py:18
  161.6 10.1 %collective-permute-start.2 = (f32[128,2,128]{2,0,1:T(8,128)S(1)}, f32[128,2,128]{2,0,1:T(8,128)S(1)}, u32[]{:S(2)}, u32[]{:S(2)}) collective-permute-start(f32[128,2,128]{2,0,1:T(8,128)S(1)} %fusion.151), channel_id=1, source_target_pairs={{0,2},{2,4},{4,6},{6,8},{8,10},{10,12},{12,14},{14,16},{16,18},{18... | collective-permute-start | bytes 393224 | tf_op jit(solution)/shard_map/while/body/eval_jaxpr/ppermute | solution.py:18
  162.0 13.9 %collective-permute-start.3 = (f32[128,2,128]{2,0,1:T(8,128)S(1)}, f32[128,2,128]{2,0,1:T(8,128)S(1)}, u32[]{:S(2)}, u32[]{:S(2)}) collective-permute-start(f32[128,2,128]{2,0,1:T(8,128)S(1)} %fusion.152), channel_id=1, source_target_pairs={{0,2},{2,4},{4,6},{6,8},{8,10},{10,12},{12,14},{14,16},{16,18},{18... | collective-permute-start | bytes 393224 | tf_op jit(solution)/shard_map/while/body/eval_jaxpr/ppermute | solution.py:18
  175.9 7.2 %collective-permute-start = (bf16[128,2,128]{2,0,1:T(8,128)(2,1)S(1)}, bf16[128,2,128]{2,0,1:T(8,128)(2,1)S(1)}, u32[]{:S(2)}, u32[]{:S(2)}) collective-permute-start(bf16[128,2,128]{2,0,1:T(8,128)(2,1)S(1)} %copy.108), channel_id=1, source_target_pairs={{0,2},{2,4},{4,6},{6,8},{8,10},{10,12},{12,14},{14,16},{16,18},{18... | collective-permute-start | bytes 196616 | tf_op jit(solution)/shard_map/while/body/eval_jaxpr/ppermute | solution.py:18
  175.9 8.0 %collective-permute-start.1 = (bf16[128,2,128]{2,0,1:T(8,128)(2,1)S(1)}, bf16[128,2,128]{2,0,1:T(8,128)(2,1)S(1)}, u32[]{:S(2)}, u32[]{:S(2)}) collective-permute-start(bf16[128,2,128]{2,0,1:T(8,128)(2,1)S(1)} %copy.109), channel_id=1, source_target_pairs={{0,2},{2,4},{4,6},{6,8},{8,10},{10,12},{12,14},{14,16},{16,18},{18... | collective-permute-start | bytes 196616 | tf_op jit(solution)/shard_map/while/body/eval_jaxpr/ppermute | solution.py:18
  181.3 8.2 %collective-permute-start.3 = (f32[128,2,128]{2,0,1:T(8,128)S(1)}, f32[128,2,128]{2,0,1:T(8,128)S(1)}, u32[]{:S(2)}, u32[]{:S(2)}) collective-permute-start(f32[128,2,128]{2,0,1:T(8,128)S(1)} %fusion.152), channel_id=1, source_target_pairs={{0,2},{2,4},{4,6},{6,8},{8,10},{10,12},{12,14},{14,16},{16,18},{18... | collective-permute-start | bytes 393224 | tf_op jit(solution)/shard_map/while/body/eval_jaxpr/ppermute | solution.py:18
  189.5 9.5 %collective-permute-start = (bf16[128,2,128]{2,0,1:T(8,128)(2,1)S(1)}, bf16[128,2,128]{2,0,1:T(8,128)(2,1)S(1)}, u32[]{:S(2)}, u32[]{:S(2)}) collective-permute-start(bf16[128,2,128]{2,0,1:T(8,128)(2,1)S(1)} %copy.108), channel_id=1, source_target_pairs={{0,2},{2,4},{4,6},{6,8},{8,10},{10,12},{12,14},{14,16},{16,18},{18... | collective-permute-start | bytes 196616 | tf_op jit(solution)/shard_map/while/body/eval_jaxpr/ppermute | solution.py:18
  189.5 9.4 %collective-permute-start.1 = (bf16[128,2,128]{2,0,1:T(8,128)(2,1)S(1)}, bf16[128,2,128]{2,0,1:T(8,128)(2,1)S(1)}, u32[]{:S(2)}, u32[]{:S(2)}) collective-permute-start(bf16[128,2,128]{2,0,1:T(8,128)(2,1)S(1)} %copy.109), channel_id=1, source_target_pairs={{0,2},{2,4},{4,6},{6,8},{8,10},{10,12},{12,14},{14,16},{16,18},{18... | collective-permute-start | bytes 196616 | tf_op jit(solution)/shard_map/while/body/eval_jaxpr/ppermute | solution.py:18
  195.1 7.9 %collective-permute-start.3 = (f32[128,2,128]{2,0,1:T(8,128)S(1)}, f32[128,2,128]{2,0,1:T(8,128)S(1)}, u32[]{:S(2)}, u32[]{:S(2)}) collective-permute-start(f32[128,2,128]{2,0,1:T(8,128)S(1)} %fusion.152), channel_id=1, source_target_pairs={{0,2},{2,4},{4,6},{6,8},{8,10},{10,12},{12,14},{14,16},{16,18},{18... | collective-permute-start | bytes 393224 | tf_op jit(solution)/shard_map/while/body/eval_jaxpr/ppermute | solution.py:18
  203.0 11.1 %collective-permute-start = (bf16[128,2,128]{2,0,1:T(8,128)(2,1)S(1)}, bf16[128,2,128]{2,0,1:T(8,128)(2,1)S(1)}, u32[]{:S(2)}, u32[]{:S(2)}) collective-permute-start(bf16[128,2,128]{2,0,1:T(8,128)(2,1)S(1)} %copy.108), channel_id=1, source_target_pairs={{0,2},{2,4},{4,6},{6,8},{8,10},{10,12},{12,14},{14,16},{16,18},{18... | collective-permute-start | bytes 196616 | tf_op jit(solution)/shard_map/while/body/eval_jaxpr/ppermute | solution.py:18
  203.0 11.1 %collective-permute-start.1 = (bf16[128,2,128]{2,0,1:T(8,128)(2,1)S(1)}, bf16[128,2,128]{2,0,1:T(8,128)(2,1)S(1)}, u32[]{:S(2)}, u32[]{:S(2)}) collective-permute-start(bf16[128,2,128]{2,0,1:T(8,128)(2,1)S(1)} %copy.109), channel_id=1, source_target_pairs={{0,2},{2,4},{4,6},{6,8},{8,10},{10,12},{12,14},{14,16},{16,18},{18... | collective-permute-start | bytes 196616 | tf_op jit(solution)/shard_map/while/body/eval_jaxpr/ppermute | solution.py:18
  217.4 8.5 %collective-permute-start = (bf16[128,2,128]{2,0,1:T(8,128)(2,1)S(1)}, bf16[128,2,128]{2,0,1:T(8,128)(2,1)S(1)}, u32[]{:S(2)}, u32[]{:S(2)}) collective-permute-start(bf16[128,2,128]{2,0,1:T(8,128)(2,1)S(1)} %copy.108), channel_id=1, source_target_pairs={{0,2},{2,4},{4,6},{6,8},{8,10},{10,12},{12,14},{14,16},{16,18},{18... | collective-permute-start | bytes 196616 | tf_op jit(solution)/shard_map/while/body/eval_jaxpr/ppermute | solution.py:18
  217.4 8.5 %collective-permute-start.1 = (bf16[128,2,128]{2,0,1:T(8,128)(2,1)S(1)}, bf16[128,2,128]{2,0,1:T(8,128)(2,1)S(1)}, u32[]{:S(2)}, u32[]{:S(2)}) collective-permute-start(bf16[128,2,128]{2,0,1:T(8,128)(2,1)S(1)} %copy.109), channel_id=1, source_target_pairs={{0,2},{2,4},{4,6},{6,8},{8,10},{10,12},{12,14},{14,16},{16,18},{18... | collective-permute-start | bytes 196616 | tf_op jit(solution)/shard_map/while/body/eval_jaxpr/ppermute | solution.py:18
  224.4 8.2 %collective-permute-start.3 = (f32[128,2,128]{2,0,1:T(8,128)S(1)}, f32[128,2,128]{2,0,1:T(8,128)S(1)}, u32[]{:S(2)}, u32[]{:S(2)}) collective-permute-start(f32[128,2,128]{2,0,1:T(8,128)S(1)} %fusion.152), channel_id=1, source_target_pairs={{0,2},{2,4},{4,6},{6,8},{8,10},{10,12},{12,14},{14,16},{16,18},{18... | collective-permute-start | bytes 393224 | tf_op jit(solution)/shard_map/while/body/eval_jaxpr/ppermute | solution.py:18
  237.9 8.2 %collective-permute-start.3 = (f32[128,2,128]{2,0,1:T(8,128)S(1)}, f32[128,2,128]{2,0,1:T(8,128)S(1)}, u32[]{:S(2)}, u32[]{:S(2)}) collective-permute-start(f32[128,2,128]{2,0,1:T(8,128)S(1)} %fusion.152), channel_id=1, source_target_pairs={{0,2},{2,4},{4,6},{6,8},{8,10},{10,12},{12,14},{14,16},{16,18},{18... | collective-permute-start | bytes 393224 | tf_op jit(solution)/shard_map/while/body/eval_jaxpr/ppermute | solution.py:18
  251.4 8.2 %collective-permute-start.3 = (f32[128,2,128]{2,0,1:T(8,128)S(1)}, f32[128,2,128]{2,0,1:T(8,128)S(1)}, u32[]{:S(2)}, u32[]{:S(2)}) collective-permute-start(f32[128,2,128]{2,0,1:T(8,128)S(1)} %fusion.152), channel_id=1, source_target_pairs={{0,2},{2,4},{4,6},{6,8},{8,10},{10,12},{12,14},{14,16},{16,18},{18... | collective-permute-start | bytes 393224 | tf_op jit(solution)/shard_map/while/body/eval_jaxpr/ppermute | solution.py:18
  264.9 8.2 %collective-permute-start.3 = (f32[128,2,128]{2,0,1:T(8,128)S(1)}, f32[128,2,128]{2,0,1:T(8,128)S(1)}, u32[]{:S(2)}, u32[]{:S(2)}) collective-permute-start(f32[128,2,128]{2,0,1:T(8,128)S(1)} %fusion.152), channel_id=1, source_target_pairs={{0,2},{2,4},{4,6},{6,8},{8,10},{10,12},{12,14},{14,16},{16,18},{18... | collective-permute-start | bytes 393224 | tf_op jit(solution)/shard_map/while/body/eval_jaxpr/ppermute | solution.py:18
  278.5 8.2 %collective-permute-start.3 = (f32[128,2,128]{2,0,1:T(8,128)S(1)}, f32[128,2,128]{2,0,1:T(8,128)S(1)}, u32[]{:S(2)}, u32[]{:S(2)}) collective-permute-start(f32[128,2,128]{2,0,1:T(8,128)S(1)} %fusion.152), channel_id=1, source_target_pairs={{0,2},{2,4},{4,6},{6,8},{8,10},{10,12},{12,14},{14,16},{16,18},{18... | collective-permute-start | bytes 393224 | tf_op jit(solution)/shard_map/while/body/eval_jaxpr/ppermute | solution.py:18
  292.0 8.2 %collective-permute-start.3 = (f32[128,2,128]{2,0,1:T(8,128)S(1)}, f32[128,2,128]{2,0,1:T(8,128)S(1)}, u32[]{:S(2)}, u32[]{:S(2)}) collective-permute-start(f32[128,2,128]{2,0,1:T(8,128)S(1)} %fusion.152), channel_id=1, source_target_pairs={{0,2},{2,4},{4,6},{6,8},{8,10},{10,12},{12,14},{14,16},{16,18},{18... | collective-permute-start | bytes 393224 | tf_op jit(solution)/shard_map/while/body/eval_jaxpr/ppermute | solution.py:18
  305.5 8.2 %collective-permute-start.3 = (f32[128,2,128]{2,0,1:T(8,128)S(1)}, f32[128,2,128]{2,0,1:T(8,128)S(1)}, u32[]{:S(2)}, u32[]{:S(2)}) collective-permute-start(f32[128,2,128]{2,0,1:T(8,128)S(1)} %fusion.152), channel_id=1, source_target_pairs={{0,2},{2,4},{4,6},{6,8},{8,10},{10,12},{12,14},{14,16},{16,18},{18... | collective-permute-start | bytes 393224 | tf_op jit(solution)/shard_map/while/body/eval_jaxpr/ppermute | solution.py:18
  319.1 8.2 %collective-permute-start.3 = (f32[128,2,128]{2,0,1:T(8,128)S(1)}, f32[128,2,128]{2,0,1:T(8,128)S(1)}, u32[]{:S(2)}, u32[]{:S(2)}) collective-permute-start(f32[128,2,128]{2,0,1:T(8,128)S(1)} %fusion.152), channel_id=1, source_target_pairs={{0,2},{2,4},{4,6},{6,8},{8,10},{10,12},{12,14},{14,16},{16,18},{18... | collective-permute-start | bytes 393224 | tf_op jit(solution)/shard_map/while/body/eval_jaxpr/ppermute | solution.py:18
  332.6 8.2 %collective-permute-start.3 = (f32[128,2,128]{2,0,1:T(8,128)S(1)}, f32[128,2,128]{2,0,1:T(8,128)S(1)}, u32[]{:S(2)}, u32[]{:S(2)}) collective-permute-start(f32[128,2,128]{2,0,1:T(8,128)S(1)} %fusion.152), channel_id=1, source_target_pairs={{0,2},{2,4},{4,6},{6,8},{8,10},{10,12},{12,14},{14,16},{16,18},{18... | collective-permute-start | bytes 393224 | tf_op jit(solution)/shard_map/while/body/eval_jaxpr/ppermute | solution.py:18
  346.1 8.2 %collective-permute-start.3 = (f32[128,2,128]{2,0,1:T(8,128)S(1)}, f32[128,2,128]{2,0,1:T(8,128)S(1)}, u32[]{:S(2)}, u32[]{:S(2)}) collective-permute-start(f32[128,2,128]{2,0,1:T(8,128)S(1)} %fusion.152), channel_id=1, source_target_pairs={{0,2},{2,4},{4,6},{6,8},{8,10},{10,12},{12,14},{14,16},{16,18},{18... | collective-permute-start | bytes 393224 | tf_op jit(solution)/shard_map/while/body/eval_jaxpr/ppermute | solution.py:18
  357.9 8.0 %collective-permute-start.4 = (f32[128,2,128]{2,0,1:T(8,128)S(1)}, f32[128,2,128]{2,0,1:T(8,128)S(1)}, u32[]{:S(2)}, u32[]{:S(2)}) collective-permute-start(f32[128,2,128]{2,0,1:T(8,128)S(1)} %fusion.49), channel_id=1, source_target_pairs={{0,2},{2,4},{4,6},{6,8},{8,10},{10,12},{12,14},{14,16},{16,18},{18... | collective-permute-start | bytes 393224 | tf_op jit(solution)/shard_map/ppermute | solution.py:18
  358.3 7.5 %collective-permute-start.5 = (bf16[128,2,128]{2,0,1:T(8,128)(2,1)S(1)}, bf16[128,2,128]{2,0,1:T(8,128)(2,1)S(1)}, u32[]{:S(2)}, u32[]{:S(2)}) collective-permute-start(bf16[128,2,128]{2,0,1:T(8,128)(2,1)S(1)} %fusion.50), channel_id=1, source_target_pairs={{0,2},{2,4},{4,6},{6,8},{8,10},{10,12},{12,14},{14,16},{16,18},{18... | collective-permute-start | bytes 196616 | tf_op jit(solution)/shard_map/ppermute | solution.py:18
  (50 other events, 327.8 us)
Sparse Core Ops, SparseCore 0:
  10.2 40.5 all-gather.2
  53.1 126.1 all-gather.4
where the time goes:
time: 397 us; the launch traced here: 393 us
  waiting for transfers between devices  151 us (38%)
  matrix products  77.2 us (19%)
  local copies, waits for them, and re-layouts  58.1 us (15%)
  other arithmetic  57.7 us (15%)
  between operations  18.6 us (5%)
  starting transfers between devices  17.7 us (4%)
  loops' own time  12.8 us (3%)
    ppermute x62, waiting for transfers between devices, shifted(): return lax.ppermute(value, axis, pairs)  121 us
    all_gather x1, waiting for transfers between devices, body(): key_piece = lax.all_gather(keys, 'seq', axis=0, tiled=True)  28.8 us
    dynamic_slice x32, local copies, waits for them, and re-layouts, body(): lax.scan(absorb, zero_stats, (stacked, jnp.arange(shards, dtype=jnp.int32)))  24.6 us
    reduce_sum x32, other arithmetic, pick_blocks(): return jnp.sum(jnp.where(matched, block_order[None, :], 0), axis=1)  23.9 us
    add x32, other arithmetic, body(): my_blocks[:, None] * half_len  23.8 us
    broadcast_in_dim x32, local copies, waits for them, and re-layouts, body(): query_live = jnp.repeat(jnp.dot(my_onehot, block_mask), half_len, axis=0)  21.9 us
    dot_general x32, matrix products, score_block(): jnp.einsum('qkgd,tkd->kgqt', query_part, keys_here, preferred_element_typ...  21.4 us
    ppermute x62, starting transfers between devices, shifted(): return lax.ppermute(value, axis, pairs)  17.6 us
  transfers between devices with their start and end apart: 65, of which 54 were waited for; matrix products, arithmetic and copies ran while one was open for 44% of the time, Pallas kernels for 0%

commit v1 on v0

v1 whole, which is shorter than its diff:
```python
import functools

import jax
import jax.numpy as jnp
from jax import lax
from jax.experimental import pallas as pl
from jax.experimental.pallas import tpu as pltpu
from jax.sharding import PartitionSpec as P

HQ = 14
KVH = 2
HD = 128
GROUP = HQ // KVH
CHUNK = 4
LOG2E = 1.4426950408889634


EPSILON = 1e-06
NEGATIVE = -1e30


def attention_kernel(
    order_ref,
    mask_ref,
    q_ref,
    do_ref,
    delta_ref,
    kv_ref,
    dq_ref,
    dkv_ref,
    slots,
    scores,
    dq_acc,
    acc,
):
    me = lax.axis_index("seq")
    blocks = order_ref.shape[0]
    half = q_ref.shape[0] // 2
    lanes = delta_ref.shape[2]
    tall = CHUNK * half
    scaling = HD ** (-0.5)
    factor = scaling * LOG2E
    width = KVH * HD
    acc[...] = jnp.zeros_like(acc)

    row = lax.broadcasted_iota(jnp.int32, (tall, lanes), 0)
    query_at = lax.rem(lax.broadcasted_iota(jnp.int32, (tall, lanes), 1), half)
    ahead = (row < half) & (row > query_at)

    for b in range(2):
        own = 2 * me + b
        query_block = order_ref[own]
        slots[0] = own

        def collect(slot, count):
            key_block = order_ref[slot]
            live = (mask_ref[query_block, key_block] == 1) & (key_block < query_block)
            slots[count] = slot
            return count + live.astype(jnp.int32)

        count = lax.fori_loop(0, blocks, collect, jnp.int32(1))
        for extra in range(CHUNK):
            slots[count + extra] = own
        chunks = (count + CHUNK - 1) // CHUNK

        for g in range(KVH):
            pad = jnp.zeros((lanes - GROUP * half, HD), jnp.bfloat16)

            def stacked(ref):
                parts = [
                    ref[b * half : (b + 1) * half, h * HD : (h + 1) * HD]
                    for h in range(g * GROUP, (g + 1) * GROUP)
                ]
                return jnp.concatenate(parts + [pad], axis=0)

            queries = stacked(q_ref)
            grads = stacked(do_ref)
            delta = delta_ref[2 * g + b]

            def key_rows(chunk, first_col):
                parts = [
                    kv_ref[
                        pl.ds(pl.multiple_of(slots[chunk * CHUNK + i] * half, half), half),
                        first_col : first_col + HD,
                    ]
                    for i in range(CHUNK)
                ]
                return jnp.concatenate(parts, axis=0)

            def score_pass(chunk, top):
                keys = key_rows(chunk, g * HD)
                score = lax.dot_general(
                    keys, queries, (((1,), (1,)), ((), ())), preferred_element_type=jnp.float32
                )
                limit = jnp.minimum((count - chunk * CHUNK) * half, tall)
                dead = (row >= limit) | (ahead & (chunk == 0))
                score = jnp.where(dead, NEGATIVE, score)
                scores[chunk] = score
                return jnp.maximum(top, jnp.max(score.reshape(tall // 8, 8, lanes), axis=0))

            top = lax.fori_loop(
                0, chunks, score_pass, jnp.full((8, lanes), NEGATIVE, jnp.float32)
            )
            top = jnp.max(top, axis=0, keepdims=True)

            def exp_pass(chunk, total):
                spread = jnp.exp2((scores[chunk] - top) * factor)
                scores[chunk] = spread
                return total + jnp.sum(spread.reshape(tall // 8, 8, lanes), axis=0)

            total = lax.fori_loop(0, chunks, exp_pass, jnp.zeros((8, lanes), jnp.float32))
            inverse = 1.0 / jnp.sum(total, axis=0, keepdims=True)
            dq_acc[...] = jnp.zeros_like(dq_acc)

            def grad_pass(chunk, carry):
                keys = key_rows(chunk, g * HD)
                vals = key_rows(chunk, width + g * HD)
                prob = scores[chunk] * inverse
                value_add = jnp.dot(
                    prob.astype(jnp.bfloat16), grads, preferred_element_type=jnp.float32
                )
                prob_grad = lax.dot_general(
                    vals, grads, (((1,), (1,)), ((), ())), preferred_element_type=jnp.float32
                )
                score_grad = (prob * (prob_grad - delta)).astype(jnp.bfloat16)
                key_add = (
                    jnp.dot(score_grad, queries, preferred_element_type=jnp.float32) * scaling
                )
                dq_acc[...] += lax.dot_general(
                    keys, score_grad, (((0,), (0,)), ((), ())), preferred_element_type=jnp.float32
                )
                for i in range(CHUNK):
                    here = pl.ds(pl.multiple_of(slots[chunk * CHUNK + i] * half, half), half)
                    part = slice(i * half, (i + 1) * half)
                    acc[here, g * HD : (g + 1) * HD] += key_add[part]
                    acc[here, width + g * HD : width + (g + 1) * HD] += value_add[part]
                return carry

            lax.fori_loop(0, chunks, grad_pass, 0)
            turned = (jnp.transpose(dq_acc[...]) * scaling).astype(jnp.bfloat16)
            for j in range(GROUP):
                h = g * GROUP + j
                dq_ref[b * half : (b + 1) * half, h * HD : (h + 1) * HD] = turned[
                    j * half : (j + 1) * half
                ]
    dkv_ref[...] = acc[...].astype(dkv_ref.dtype)


def attention_grads(order, mask, queries, out_grad, row_delta, kv):
    rows = queries.shape[0]
    half = rows // 2
    keys = kv.shape[0]
    lanes = -(-GROUP * half // 128) * 128
    blocks = order.shape[0]
    delta = jnp.transpose(row_delta.reshape(2, half, KVH, GROUP), (2, 0, 3, 1))
    delta = delta.reshape(2 * KVH, 1, GROUP * half)
    delta = jnp.pad(delta, ((0, 0), (0, 0), (0, lanes - GROUP * half)))
    max_chunks = -(-blocks // CHUNK)
    smem = pl.BlockSpec(memory_space=pltpu.SMEM)
    vmem = pl.BlockSpec(memory_space=pltpu.VMEM)
    return pl.pallas_call(
        attention_kernel,
        out_shape=(
            jax.ShapeDtypeStruct((rows, HQ * HD), jnp.bfloat16),
            jax.ShapeDtypeStruct((keys, 2 * KVH * HD), jnp.bfloat16),
        ),
        in_specs=[smem, smem, vmem, vmem, vmem, vmem],
        out_specs=(vmem, vmem),
        scratch_shapes=[
            pltpu.SMEM((blocks + CHUNK + 1,), jnp.int32),
            pltpu.VMEM((max_chunks, CHUNK * half, lanes), jnp.float32),
            pltpu.VMEM((HD, lanes), jnp.float32),
            pltpu.VMEM((keys, 2 * KVH * HD), jnp.float32),
        ],
        cost_estimate=pl.CostEstimate(
            flops=5 * rows * keys * HQ * HD,
            bytes_accessed=4 * keys * KVH * HD * 2 + 3 * rows * HQ * HD * 2,
            transcendentals=rows * keys * HQ // 2,
        ),
        compiler_params=pltpu.CompilerParams(vmem_limit_bytes=48 * 1024 * 1024),
        name="attention_grads",
    )(order, mask, queries, out_grad, delta, kv)


def shifted(value, axis, steps):
    count = lax.axis_size(axis)
    pairs = [(source, (source + steps) % count) for source in range(count)]
    return lax.ppermute(value, axis, pairs)


def swapped(array, axis, apart):
    return lax.ppermute(array, axis, [(i, i ^ 1 << apart) for i in range(lax.axis_size(axis))])


def body(
    queries,
    keys,
    values,
    out_grad,
    row_delta,
    layer_input,
    norm_gain,
    qkv_weight,
    block_order,
    block_mask,
    frame_owner,
    vision_features,
    post_gain,
    projector,
):
    tok_rows = queries.shape[0]
    half_len = tok_rows // 2
    my_index = lax.axis_index("seq")
    my_blocks = lax.dynamic_slice_in_dim(block_order, 2 * my_index, 2, 0)
    kv = lax.all_gather(jnp.concatenate([keys, values], axis=1), "seq", axis=0, tiled=True)
    query_grad, kv_part = attention_grads(
        block_order, block_mask, queries, out_grad, row_delta, kv
    )
    kv_grad = lax.psum_scatter(kv_part, "seq", scatter_dimension=0, tiled=True)
    head_grads = jnp.concatenate([query_grad, kv_grad], axis=1)
    norm_grad = jnp.dot(
        head_grads,
        lax.all_gather(qkv_weight, "seq", axis=0, tiled=True).T,
        preferred_element_type=jnp.float32,
    ).astype(jnp.bfloat16)
    inputs = layer_input.astype(jnp.float32)
    inverse = lax.rsqrt(jnp.mean(inputs * inputs, axis=1, keepdims=True) + EPSILON)
    scaled = norm_grad.astype(jnp.float32) * norm_gain
    token_grad = (
        inverse * scaled - inputs * inverse**3 * jnp.mean(scaled * inputs, axis=1, keepdims=True)
    ).astype(jnp.bfloat16)
    frame_table = jnp.arange(frame_owner.shape[0], dtype=jnp.int32)
    my_frame = jnp.sum(jnp.where(frame_owner == my_index, frame_table, 0))
    keep_first = my_blocks[0] // 2 == my_frame
    kept_block = jnp.where(keep_first, my_blocks[0], my_blocks[1])
    leading = kept_block % 2 == 0
    halves = token_grad.reshape(2, half_len, token_grad.shape[1])
    kept = jnp.where(keep_first, halves[0], halves[1])
    sending = jnp.where(keep_first, halves[1], halves[0])
    received = swapped(sending, "seq", 0)
    frame_rows = jnp.where(
        leading,
        jnp.concatenate([kept, received], axis=0),
        jnp.concatenate([received, kept], axis=0),
    )
    post_grad = jnp.dot(frame_rows, projector.T, preferred_element_type=jnp.float32)
    features = vision_features[0].astype(jnp.float32)
    centered = features - jnp.mean(features, axis=1, keepdims=True)
    deviation = lax.rsqrt(jnp.mean(centered * centered, axis=1, keepdims=True) + EPSILON)
    normed = centered * deviation
    weighted = post_grad * post_gain
    encoder_grad = (
        deviation
        * (
            weighted
            - jnp.mean(weighted, axis=1, keepdims=True)
            - normed * jnp.mean(weighted * normed, axis=1, keepdims=True)
        )
    ).astype(jnp.bfloat16)
    return (token_grad, encoder_grad[None])


def solution(mesh):
    placed = (
        P(("batch", "seq"), None),
        P(("batch", "seq"), None),
        P(("batch", "seq"), None),
        P(("batch", "seq"), None),
        P(("batch", "seq"), None),
        P(("batch", "seq"), None),
        P(),
        P("seq", None),
        P("batch"),
        P("batch", None),
        P("batch"),
        P(("batch", "seq"), None, None),
        P(),
        P(),
    )
    return jax.shard_map(
        body,
        mesh=mesh,
        in_specs=placed,
        out_specs=(P(("batch", "seq"), None), P(("batch", "seq"), None, None)),
        check_vma=False,
    )
```

time: 397 us -> 290 us (0.73)
  waiting for transfers between devices: 151 us -> 231 us
  matrix products: 77.2 us -> 17.5 us
  other arithmetic: 57.7 us -> 5.21 us
  local copies, waits for them, and re-layouts: 58.1 us -> 6.56 us
  starting transfers between devices: 17.7 us -> 0.44 us
  loops' own time: 12.8 us -> 0 us
  Pallas kernels: 0 us -> 10.5 us
    all_gather x1, waiting for transfers between devices: 0.02 us -> 126 us  [body(): lax.all_gather(qkv_weight, 'seq', axis=0, tiled=True)]
    ppermute x62 -> x0, waiting for transfers between devices: 121 us -> none  [shifted(): return lax.ppermute(value, axis, pairs)]
    dot_general x129 -> x0, matrix products: 61.9 us -> none  [the longest x32 21.4 us: score_block(): jnp.einsum('qkgd,tkd->kgqt', query_part, keys_here, preferred_element_typ...]
    reduce_scatter x0 -> x1, waiting for transfers between devices: none -> 58.8 us  [body(): kv_grad = lax.psum_scatter(kv_part, 'seq', scatter_dimension=0, tiled=True)]
    reduce_sum x48 -> x0, other arithmetic: 26.7 us -> none  [the longest x32 23.9 us: pick_blocks(): return jnp.sum(jnp.where(matched, block_order[None, :], 0), axis=1)]
    add x81 -> x0, other arithmetic: 25 us -> none  [the longest x32 23.8 us: body(): my_blocks[:, None] * half_len]
    dynamic_slice x32 -> x1, local copies, waits for them, and re-layouts: 24.6 us -> 0.08 us  [body(): my_blocks = lax.dynamic_slice_in_dim(block_order, 2 * my_index, 2, 0)]
    broadcast_in_dim x32 -> x0, local copies, waits for them, and re-layouts: 21.9 us -> none  [body(): query_live = jnp.repeat(jnp.dot(my_onehot, block_mask), half_len, axis=0)]
  transfers between devices with their start and end apart: 65 -> 4, of which waited for: 54 -> 4; matrix products, arithmetic and copies ran while one was open for 44% -> 1% of each run, Pallas kernels for 0% -> 0%
where the time goes in v1:
time: 290 us; the launch traced here: 289 us
  waiting for transfers between devices  231 us (80%)
  between operations  17.9 us (6%)
  matrix products  17.5 us (6%)
  Pallas kernels  10.5 us (4%)
  local copies, waits for them, and re-layouts  6.56 us (2%)
  other arithmetic  5.21 us (2%)
    all_gather x1, waiting for transfers between devices, body(): lax.all_gather(qkv_weight, 'seq', axis=0, tiled=True)  126 us
    reduce_scatter x1, waiting for transfers between devices, body(): kv_grad = lax.psum_scatter(kv_part, 'seq', scatter_dimension=0, tiled=True)  58.8 us
    all_gather x1, waiting for transfers between devices, body(): lax.all_gather(jnp.concatenate([keys, values], axis=1), 'seq', axis=0, ti...  45.2 us
    dot_general x1, matrix products, body(): jnp.dot(head_grads, lax.all_gather(qkv_weight, 'seq', axis=0, tiled=True)...  11.4 us
    pallas_call x1, Pallas kernels, attention_grads(): pl.pallas_call(attention_kernel, out_shape=(jax.ShapeDtypeStruct((rows, H...  10.5 us
    dot_general x1, matrix products, body(): jnp.dot(frame_rows, projector.T, preferred_element_type=jnp.float32)  6.14 us
  transfers between devices with their start and end apart: 4, of which 4 were waited for; matrix products, arithmetic and copies ran while one was open for 1% of the time, Pallas kernels for 0%

profile of v1, /device:TPU:0, one launch (start us, length us, event | category | flops | bytes accessed | tf_op | source)
XLA Modules:
  0.0 289.0 jit_solution(5769224684468552317)
XLA Ops:
  7.2 0.0 all-gather.3.cloned.1.call-start
  7.2 1.5 pad_maximum_fusion
  8.7 0.0 all-gather.3.cloned.1.call-update
  8.8 0.0 reduce-scatter.2.cloned.1.call-start
  8.8 0.8 reshape.56
  9.6 0.1 reshape.58
  9.7 45.2 %all-gather.3.cloned.1.call-done.kv_ref = bf16[2048,512]{1,0:T(8,128)(2,1)} async-done(((bf16[128,512]{1,0:T(8,128)(2,1)}), bf16[2048,512]{1,0:T(8,128)(2,1)}) %all-gather.3.cloned.1.call-update) | async-done | bytes 2097168 | tf_op jit(solution)/shard_map/all_gather | solution.py:215
  54.9 1.6 copy-done
  56.5 1.0 copy-done.1
  57.5 1.0 copy-done.2
  58.6 0.7 copy-done.3
  59.3 0.7 copy-done.4
  59.9 10.5 %attention_grads.1 = (bf16[128,1792]{1,0:T(8,128)(2,1)S(1)}, bf16[2048,512]{1,0:T(8,128)(2,1)}) custom-call(s32[32]{0:T(128)S(1)} %copy-done.4, s32[32,32]{1,0:T(8,128)S(1)} %copy-done.3, bf16[128,1792]{1,0:T(8,128)(2,1)S(1)} %copy-done.1, bf16[128,1792]{1,0:T(8,128)(2,1)S(1)} %copy-done.2, f32[4,1,512]{2,1,0:T(1,128)S(1)} %pad.4.delta_ref, ...), custom_call_target="tpu_custom_call" | custom-call | flops 2348810240 | bytes 5570560 | tf_op jit(solution)/shard_map/attention_grads/pallas_call | solution.py:161
  70.4 0.0 reduce-scatter.2.cloned.1.call-update
  70.4 0.0 all-gather.5.cloned.1.call-start
  70.5 0.7 all-gather.5.cloned.1.call-update
  71.2 0.1 dynamic_slice.3
  71.3 0.6 fusion.31
  74.1 0.6 fusion.27
  75.4 0.1 convert_reduce_fusion
  75.5 58.8 %reduce-scatter.2.cloned.1.call-done = bf16[128,512]{1,0:T(8,128)(2,1)} async-done(((bf16[2048,512]{1,0:T(8,128)(2,1)}), bf16[128,512]{1,0:T(8,128)(2,1)}) %reduce-scatter.2.cloned.1.call-update) | async-done | bytes 131088 | tf_op jit(solution)/shard_map/reduce_scatter | solution.py:219
  134.3 126.1 %all-gather.5.cloned.1.call-done = bf16[3584,2304]{1,0:T(8,128)(2,1)} async-done(((bf16[224,2304]{1,0:T(8,128)(2,1)}), bf16[3584,2304]{1,0:T(8,128)(2,1)}) %all-gather.5.cloned.1.call-update) | async-done | bytes 16515088 | tf_op jit(solution)/shard_map/all_gather | solution.py:223
  260.4 11.4 %fusion.2 = (f32[128]{0:T(128)S(1)}, f32[128]{0:T(128)S(1)}, f32[128,3584]{1,0:T(8,128)S(1)}) fusion(bf16[128,3584]{1,0:T(8,128)(2,1)} %param.19, f32[3584]{0:T(1024)S(1)} %copy-done.8, bf16[3584,2304]{1,0:T(8,128)(2,1)} %all-gather.5.cloned.1.call-done, bf16[128,512]{1,0:T(8,128)(2,1)} %reduce-scatter.2.cloned.1.call-done, ...), kind=kOutput, calls=%fused_computation.7 | convolution fusion | flops 2118778624 | bytes 19872768 | tf_op jit(solution)/shard_map/dot_general | solution.py:221
  271.7 1.7 fusion.5
  273.4 0.0 copy-start.6
  273.4 0.0 copy-start.9
  273.4 0.1 broadcast_select_fusion.1
  273.5 0.3 collective-permute-start
  275.0 0.2 fusion.22
  275.3 0.1 collective-permute-done
  275.4 6.1 %fusion.30 = (f32[128]{0:T(128)S(1)}, f32[128]{0:T(128)S(1)}, f32[128,1152]{1,0:T(8,128)S(1)}) fusion(f32[128]{0:T(128)S(1)} %add_rsqrt_fusion, f32[128]{0:T(128)S(1)} %broadcast_multiply_fusion.2, bf16[1,128,1152]{2,1,0:T(8,128)(2,1)S(1)} %copy-done.7, f32[1152]{0:T(1024)S(1)} %copy-done.9, bf16[1152,3584]{1,0:T(8,128)(2,1)} %param.27, ...), kind=kOutput, calls=%fused_computation.50 | convolution fusion | flops 1062125312 | bytes 10066433 | tf_op jit(solution)/shard_map/dot_general | solution.py:246
  281.6 0.9 fusion.26
  (22 shorter events, 0.1 us)
Async XLA Ops:
  7.2 47.8 %all-gather.3.cloned.1.call-start = ((), (), s32[]{:S(2)}) async-start(), calls=%async_computation.1 | async-start | bytes 2228224 | tf_op jit(solution)/shard_map/all_gather | solution.py:215
  8.8 125.5 %reduce-scatter.2.cloned.1.call-start = ((), (), s32[]{:S(2)}) async-start(), calls=%async_computation.2 | async-start | bytes 2228224 | tf_op jit(solution)/shard_map/reduce_scatter | solution.py:219
  54.9 1.6 copy-start
  56.5 1.0 copy-start.1
  57.5 1.0 copy-start.2
  58.5 0.7 copy-start.3
  59.3 0.7 copy-start.4
  70.4 0.8 copy-start.5
  70.4 3.7 %copy-start.10 = (s32[16]{0:T(128)S(1)}, s32[16]{0:T(128)}, u32[]{:S(2)}) copy-start(s32[16]{0:T(128)} %param.24) | copy-start | bytes 196
  70.4 5.0 %copy-start.7 = (bf16[1,128,1152]{2,1,0:T(8,128)(2,1)S(1)}, bf16[1,128,1152]{2,1,0:T(8,128)(2,1)}, u32[]{:S(2)}) copy-start(bf16[1,128,1152]{2,1,0:T(8,128)(2,1)} %param.25) | copy-start | bytes 884740
  70.4 190.0 %copy-start.8 = (f32[3584]{0:T(1024)S(1)}, f32[3584]{0:T(1024)}, u32[]{:S(2)}) copy-start(f32[3584]{0:T(1024)} %param.20) | copy-start | bytes 43012
  70.4 189.9 %all-gather.5.cloned.1.call-start = ((), (), s32[]{:S(2)}) async-start(), calls=%async_computation.3 | async-start | bytes 17547264 | tf_op jit(solution)/shard_map/all_gather | solution.py:223
  273.4 8.1 %copy-start.6 = (bf16[128,3584]{1,0:T(8,128)(2,1)}, bf16[128,3584]{1,0:T(8,128)(2,1)S(1)}, u32[]{:S(2)}) copy-start(bf16[128,3584]{1,0:T(8,128)(2,1)S(1)} %fusion.5) | copy-start | bytes 2752516
  273.4 2.0 copy-start.9
  273.5 1.9 collective-permute-start
Sparse Core Ops, SparseCore 0:
  10.7 44.1 all-gather.2
  70.6 63.6 reduce-scatter.1
  136.6 123.7 all-gather.4

commit v2 on v1

--- a/solution.py
+++ b/solution.py
@@ -182,10 +182,340 @@
     )(order, mask, queries, out_grad, delta, kv)
 
 
-def shifted(value, axis, steps):
-    count = lax.axis_size(axis)
-    pairs = [(source, (source + steps) % count) for source in range(count)]
-    return lax.ppermute(value, axis, pairs)
+MESH = pl.DeviceIdType.MESH
+
+
+def remote(src, dst, send_sem, recv_sem, device):
+    return pltpu.make_async_remote_copy(
+        src_ref=src,
+        dst_ref=dst,
+        send_sem=send_sem,
+        recv_sem=recv_sem,
+        device_id=device,
+        device_id_type=MESH,
+    )
+
+
+def when(condition, action):
+    if condition is None:
+        action()
+    else:
+        pl.when(condition)(action)
+
+
+def places():
+    me = lax.axis_index("seq")
+    x = lax.rem(lax.axis_index("batch"), 2)
+    z, y, c = me // 4, lax.rem(me // 2, 2), lax.rem(me, 2)
+    return me, x, z, y, c
+
+
+def gather_kernel(
+    depth,
+    kv_ref,
+    w_ref,
+    kv_all,
+    w_all,
+    own_sem,
+    kv_recv,
+    kv_core_recv,
+    kv_up,
+    kv_down,
+    kv_y,
+    kv_core,
+    w_recv,
+    w_x_recv,
+    w_core_recv,
+    w_cx_recv,
+    w_up,
+    w_down,
+    w_y,
+    w_x,
+    w_core,
+    w_cx,
+):
+    me, x, z, y, c = places()
+    rows = w_ref.shape[0]
+    part = 5 * (rows // 16) // 14 * 16
+    up, down = {"seq": me + 4}, {"seq": me - 4}
+    beside, core = {"seq": me + 2 - 4 * y}, {"seq": me + 1 - 2 * c}
+    across = {"batch": lax.axis_index("batch") + 1 - 2 * x}
+    has_up, has_down = z < depth - 1, z > 0
+
+    barrier = pltpu.get_barrier_semaphore()
+    for peer, present in (
+        (up, has_up),
+        (down, has_down),
+        (beside, None),
+        (core, None),
+        (across, None),
+    ):
+        when(
+            present,
+            lambda peer=peer: pl.semaphore_signal(
+                barrier, inc=1, device_id=peer, device_id_type=MESH
+            ),
+        )
+    pl.semaphore_wait(barrier, 3 + has_up.astype(jnp.int32) + has_down.astype(jnp.int32))
+
+    started = []
+
+    def start(copy, condition=None):
+        when(condition, copy.start)
+        started.append((condition, copy))
+
+    def both(first, second):
+        return second if first is None else jnp.logical_and(first, second)
+
+    def line(step):
+        if step == 0:
+            return [(z, None, None)]
+        return [(z - step, z - step >= 0, True), (z + step, z + step < depth, False)]
+
+    def slot(j, side):
+        return 2 * j + side
+
+    own_kv = pltpu.make_async_copy(kv_ref, kv_all.at[me], own_sem.at[0])
+    own_w = pltpu.make_async_copy(w_ref, w_all.at[me], own_sem.at[1])
+
+    def kv_at(u):
+        return kv_all.at[2 * u + c]
+
+    def kv_pass(j, condition, upward, first):
+        u = slot(j, y)
+        src = kv_ref if first else kv_at(u)
+        if upward is not False:
+            start(remote(src, kv_at(u), kv_up.at[j], kv_recv.at[u], up), both(condition, has_up))
+        if upward is not True:
+            start(
+                remote(src, kv_at(u), kv_down.at[j], kv_recv.at[u], down),
+                both(condition, has_down),
+            )
+        start(remote(src, kv_at(u), kv_y.at[j], kv_recv.at[u], beside), condition)
+        start(remote(src, kv_at(u), kv_core.at[u], kv_core_recv.at[u], core), condition)
+
+    def arrived(ref, semaphore, condition=None):
+        when(condition, remote(ref, ref, own_sem.at[2], semaphore, core).wait_recv)
+
+    def safe(j):
+        return jnp.clip(j, 0, depth - 1)
+
+    kv_pass(z, None, None, True)
+    own_kv.start()
+    own_w.start()
+    for step in range(1, depth):
+        for j, condition, upward in line(step):
+            j = safe(j)
+            arrived(kv_at(slot(j, y)), kv_recv.at[slot(j, y)], condition)
+            kv_pass(j, condition, upward, False)
+
+    main = pl.ds(pl.multiple_of(x * part, 16), rows - part)
+    mine = pl.ds(pl.multiple_of(x * (rows - part), 16), part)
+    other = pl.ds(pl.multiple_of((1 - x) * (rows - part), 16), part)
+
+    def w_at(u, which):
+        return w_all.at[2 * u + c, which]
+
+    def w_pass(j, condition, upward, first):
+        u = slot(j, y)
+        src = w_ref.at[main] if first else w_at(u, main)
+        dst = w_at(u, main)
+        if upward is not False:
+            start(remote(src, dst, w_up.at[j], w_recv.at[u], up), both(condition, has_up))
+        if upward is not True:
+            start(remote(src, dst, w_down.at[j], w_recv.at[u], down), both(condition, has_down))
+        start(remote(src, dst, w_y.at[j], w_recv.at[u], beside), condition)
+
+    def w_share(u, condition):
+        start(
+            remote(w_at(u, mine), w_at(u, mine), w_x.at[u], w_x_recv.at[u], across), condition
+        )
+        start(
+            remote(w_at(u, main), w_at(u, main), w_core.at[u], w_core_recv.at[u], core), condition
+        )
+
+    def w_finish(u, condition):
+        arrived(w_at(u, other), w_x_recv.at[u], condition)
+        start(
+            remote(w_at(u, other), w_at(u, other), w_cx.at[u], w_cx_recv.at[u], core), condition
+        )
+
+    w_pass(z, None, None, True)
+    own_u = slot(z, y)
+    start(
+        remote(w_ref.at[main], w_at(own_u, main), w_core.at[own_u], w_core_recv.at[own_u], core)
+    )
+    start(remote(w_ref.at[other], w_at(own_u, other), w_cx.at[own_u], w_cx_recv.at[own_u], core))
+
+    for step in range(depth):
+        for j, condition, _ in line(step):
+            u = slot(safe(j), 1 - y)
+            arrived(kv_at(u), kv_recv.at[u], condition)
+            start(remote(kv_at(u), kv_at(u), kv_core.at[u], kv_core_recv.at[u], core), condition)
+
+    waiting = []
+    for step in range(1, depth + 1):
+        shared = []
+        if step < depth:
+            for j, condition, upward in line(step):
+                j = safe(j)
+                u = slot(j, y)
+                arrived(w_at(u, main), w_recv.at[u], condition)
+                w_pass(j, condition, upward, False)
+                w_share(u, condition)
+                shared.append((u, condition))
+        for j, condition, _ in line(step - 1):
+            u = slot(safe(j), 1 - y)
+            arrived(w_at(u, main), w_recv.at[u], condition)
+            w_share(u, condition)
+            shared.append((u, condition))
+        for u, condition in waiting:
+            w_finish(u, condition)
+        waiting = shared
+    for u, condition in waiting:
+        w_finish(u, condition)
+
+    for u in range(2 * depth):
+        from_core = 2 * u + 1 - c
+        arrived(kv_all.at[from_core], kv_core_recv.at[u])
+        arrived(w_all.at[from_core, main], w_core_recv.at[u])
+        arrived(w_all.at[from_core, other], w_cx_recv.at[u])
+    for condition, copy in started:
+        when(condition, copy.wait_send)
+    own_kv.wait()
+    own_w.wait()
+
+
+def gather(kv, weight, count):
+    depth = count // 4
+    line, pairs = pltpu.SemaphoreType.DMA((depth,)), pltpu.SemaphoreType.DMA((2 * depth,))
+    anywhere = pl.BlockSpec(memory_space=pl.ANY)
+    vmem = pl.BlockSpec(memory_space=pltpu.VMEM)
+    return pl.pallas_call(
+        functools.partial(gather_kernel, depth),
+        out_shape=(
+            jax.ShapeDtypeStruct((count,) + kv.shape, kv.dtype),
+            jax.ShapeDtypeStruct((count,) + weight.shape, weight.dtype),
+        ),
+        in_specs=[vmem, vmem],
+        out_specs=(anywhere, anywhere),
+        scratch_shapes=[pltpu.SemaphoreType.DMA((3,))]
+        + [pairs, pairs, line, line, line, pairs]
+        + [pairs, pairs, pairs, pairs, line, line, line, pairs, pairs, pairs],
+        compiler_params=pltpu.CompilerParams(collective_id=0, has_side_effects=True),
+        name="gather",
+    )(kv, weight)
+
+
+def reduce_kernel(
+    depth,
+    part_ref,
+    out_ref,
+    core_in,
+    sum_out,
+    y_in,
+    z_in,
+    core_send,
+    core_recv,
+    y_send,
+    y_recv,
+    z_send,
+    z_recv,
+):
+    me, x, z, y, c = places()
+    beside, core = {"seq": me + 2 - 4 * y}, {"seq": me + 1 - 2 * c}
+
+    def far(k):
+        return lax.rem(z + k, depth)
+
+    barrier = pltpu.get_barrier_semaphore()
+    peers = [beside, core] + [{"seq": 4 * far(k) + 2 * y + c} for k in range(1, depth)]
+    for peer in peers:
+        pl.semaphore_signal(barrier, inc=1, device_id=peer, device_id_type=MESH)
+    pl.semaphore_wait(barrier, len(peers))
+
+    def wide(ref):
+        return ref[...].astype(jnp.float32)
+
+    order = list(range(1, depth)) + [0]
+    started = []
+
+    def start(copy):
+        copy.start()
+        started.append(copy)
+
+    core_copies, y_copies = {}, {}
+    for side in (1, 0):
+        for k in order:
+            u = 2 * far(k) + (y if side == 0 else 1 - y)
+            copy = remote(
+                part_ref.at[2 * u + 1 - c], core_in.at[u], core_send.at[u], core_recv.at[u], core
+            )
+            start(copy)
+            core_copies[side, k] = (copy, u)
+
+    def arrived(ref, send_semaphore, semaphore, device):
+        remote(ref, ref, send_semaphore, semaphore, device).wait_recv()
+
+    for k in order:
+        j = far(k)
+        u = 2 * j + 1 - y
+        arrived(core_in.at[u], core_send.at[u], core_recv.at[u], core)
+        total = wide(part_ref.at[2 * u + c]) + wide(core_in.at[u])
+        sum_out[u] = total.astype(sum_out.dtype)
+        start(remote(sum_out.at[u], y_in.at[j], y_send.at[j], y_recv.at[j], beside))
+    for k in order:
+        j = far(k)
+        u = 2 * j + y
+        arrived(core_in.at[u], core_send.at[u], core_recv.at[u], core)
+        total = wide(part_ref.at[2 * u + c]) + wide(core_in.at[u])
+        arrived(y_in.at[j], y_send.at[j], y_recv.at[j], beside)
+        total = total + wide(y_in.at[j])
+        if k != 0:
+            sum_out[u] = total.astype(sum_out.dtype)
+            start(
+                remote(
+                    sum_out.at[u],
+                    z_in.at[z],
+                    z_send.at[j],
+                    z_recv.at[z],
+                    {"seq": 4 * j + 2 * y + c},
+                )
+            )
+    for k in range(1, depth):
+        j = far(k)
+        arrived(z_in.at[j], z_send.at[j], z_recv.at[j], core)
+        total = total + wide(z_in.at[j])
+    out_ref[...] = total.astype(out_ref.dtype)
+    for copy in started:
+        copy.wait_send()
+
+
+def reduce_shards(parts, count):
+    depth = count // 4
+    block = parts.shape[1:]
+    line, pairs = pltpu.SemaphoreType.DMA((depth,)), pltpu.SemaphoreType.DMA((2 * depth,))
+    vmem = pl.BlockSpec(memory_space=pltpu.VMEM)
+    return pl.pallas_call(
+        functools.partial(reduce_kernel, depth),
+        out_shape=jax.ShapeDtypeStruct(block, parts.dtype),
+        in_specs=[vmem],
+        out_specs=vmem,
+        scratch_shapes=[
+            pltpu.VMEM((2 * depth,) + block, parts.dtype),
+            pltpu.VMEM((2 * depth,) + block, parts.dtype),
+            pltpu.VMEM((depth,) + block, parts.dtype),
+            pltpu.VMEM((depth,) + block, parts.dtype),
+            pairs,
+            pairs,
+            line,
+            line,
+            line,
+            line,
+        ],
+        compiler_params=pltpu.CompilerParams(collective_id=1, has_side_effects=True),
+        name="reduce_shards",
+    )(parts)
 
 
 def swapped(array, axis, apart):
@@ -212,15 +542,18 @@
     half_len = tok_rows // 2
     my_index = lax.axis_index("seq")
     my_blocks = lax.dynamic_slice_in_dim(block_order, 2 * my_index, 2, 0)
-    kv = lax.all_gather(jnp.concatenate([keys, values], axis=1), "seq", axis=0, tiled=True)
+    count = lax.axis_size("seq")
+    kv_all, weight_all = gather(jnp.concatenate([keys, values], axis=1), qkv_weight, count)
+    kv = kv_all.reshape(count * tok_rows, kv_all.shape[2])
+    weight = weight_all.reshape(count * qkv_weight.shape[0], qkv_weight.shape[1])
     query_grad, kv_part = attention_grads(
         block_order, block_mask, queries, out_grad, row_delta, kv
     )
-    kv_grad = lax.psum_scatter(kv_part, "seq", scatter_dimension=0, tiled=True)
+    kv_grad = reduce_shards(kv_part.reshape(kv_all.shape), count)
     head_grads = jnp.concatenate([query_grad, kv_grad], axis=1)
     norm_grad = jnp.dot(
         head_grads,
-        lax.all_gather(qkv_weight, "seq", axis=0, tiled=True).T,
+        weight.T,
         preferred_element_type=jnp.float32,
     ).astype(jnp.bfloat16)
     inputs = layer_input.astype(jnp.float32)

time: 290 us -> 163 us (0.56)
  waiting for transfers between devices: 231 us -> 0.01 us
  Pallas kernels: 10.5 us -> 124 us
  between operations: 17.9 us -> 5.3 us
  local copies, waits for them, and re-layouts: 6.56 us -> 9.6 us
    all_gather x2 -> x0, waiting for transfers between devices: 171 us -> none  [the longest x1 126 us: body(): lax.all_gather(qkv_weight, 'seq', axis=0, tiled=True)]
    pallas_call x0 -> x2, Pallas kernels: none -> 114 us  [the longest x1 90.1 us: gather(): pl.pallas_call(functools.partial(gather_kernel, depth), out_shape=(jax.Sh...]
    reduce_scatter x1 -> x0, waiting for transfers between devices: 58.8 us -> none  [body(): kv_grad = lax.psum_scatter(kv_part, 'seq', scatter_dimension=0, tiled=True)]
  transfers between devices with their start and end apart: 4 -> 1, of which waited for: 4 -> 0; matrix products, arithmetic and copies ran while one was open for 1% -> 0% of each run, Pallas kernels for 0% -> 0%
where the time goes in v2:
time: 163 us; the launch traced here: 162 us
  Pallas kernels  124 us (76%)
  matrix products  17.5 us (11%)
  local copies, waits for them, and re-layouts  9.6 us (6%)
  between operations  5.3 us (3%)
  other arithmetic  5.22 us (3%)
    pallas_call x1, Pallas kernels, gather(): pl.pallas_call(functools.partial(gather_kernel, depth), out_shape=(jax.Sh...  90.1 us
    pallas_call x1, Pallas kernels, reduce_shards(): pl.pallas_call(functools.partial(reduce_kernel, depth), out_shape=jax.Sha...  23.4 us
    dot_general x1, matrix products, body(): jnp.dot(head_grads, weight.T, preferred_element_type=jnp.float32)  11.4 us
    pallas_call x1, Pallas kernels, attention_grads(): pl.pallas_call(attention_kernel, out_shape=(jax.ShapeDtypeStruct((rows, H...  10.7 us
    unnamed x22, local copies, waits for them, and re-layouts  7.35 us
    dot_general x1, matrix products, body(): jnp.dot(frame_rows, projector.T, preferred_element_type=jnp.float32)  6.15 us
  transfers between devices with their start and end apart: 1, of which 0 were waited for; matrix products, arithmetic and copies ran while one was open for 0% of the time, Pallas kernels for 0%

profile of v2, /device:TPU:0, one launch (start us, length us, event | category | flops | bytes accessed | tf_op | source)
XLA Modules:
  0.0 162.0 jit_solution(15210185340377067908)
XLA Ops:
  0.6 0.7 dynamic_slice.3
  1.4 0.6 fusion.31
  4.5 0.8 reshape.65
  5.3 0.1 reshape.70
  5.4 1.5 pad_maximum_fusion.kv_ref
  7.0 90.1 %gather.1 = (bf16[16,128,512]{2,1,0:T(8,128)(2,1)}, bf16[16,224,2304]{2,1,0:T(8,128)(2,1)}) custom-call(bf16[128,512]{1,0:T(8,128)(2,1)} %pad_maximum_fusion.kv_ref, bf16[224,2304]{1,0:T(8,128)(2,1)} %w_ref.1), custom_call_target="tpu_custom_call" | custom-call | tf_op jit(solution)/shard_map/gather/pallas_call | solution.py:394
  97.1 0.0 copy-start.1
  97.1 1.6 copy-done.1
  98.7 1.0 copy-done.2
  99.7 1.0 copy-done.3
  100.8 0.7 copy-done.4
  101.5 0.7 copy-done.5
  102.1 10.7 %attention_grads.1 = (bf16[128,1792]{1,0:T(8,128)(2,1)S(1)}, bf16[2048,512]{1,0:T(8,128)(2,1)S(1)}) custom-call(s32[32]{0:T(128)S(1)} %copy-done.5, s32[32,32]{1,0:T(8,128)S(1)} %copy-done.4, bf16[128,1792]{1,0:T(8,128)(2,1)S(1)} %copy-done.2, bf16[128,1792]{1,0:T(8,128)(2,1)S(1)} %copy-done.3, f32[4,1,512]{2,1,0:T(1,128)S(1)} %pad.4.delta_ref, ...), custom_call_target="tpu_custom_call" | custom-call | flops 2348810240 | bytes 5570560 | tf_op jit(solution)/shard_map/attention_grads/pallas_call | solution.py:161
  112.8 0.0 copy-start
  112.9 1.3 copy-done
  114.2 23.4 %reduce_shards.1 = bf16[128,512]{1,0:T(8,128)(2,1)} custom-call(bf16[16,128,512]{2,1,0:T(8,128)(2,1)} %bitcast.38), custom_call_target="tpu_custom_call" | custom-call | tf_op jit(solution)/shard_map/reduce_shards/pallas_call | solution.py:499
  137.6 0.0 copy-done.10
  137.6 0.6 fusion.27
  138.3 0.0 copy-done.8
  138.3 11.4 %fusion.2 = (f32[128]{0:T(128)S(1)}, f32[128]{0:T(128)S(1)}, f32[128,3584]{1,0:T(8,128)S(1)}) fusion(bf16[128,3584]{1,0:T(8,128)(2,1)} %param.19, f32[3584]{0:T(1024)S(1)} %copy-done.8, bf16[3584,2304]{1,0:T(8,128)(2,1)} %bitcast.40, bf16[128,512]{1,0:T(8,128)(2,1)} %reduce_shards.1, bf16[128,1792]{1,0:T(8,128)(2,1)S(1)} %get-tuple-element.7), kind=kOutput, calls=%fused_computation.7 | convolution fusion | flops 2118778624 | bytes 19872768 | tf_op jit(solution)/shard_map/dot_general | solution.py:554
  150.3 1.6 %fusion.5 = bf16[128,3584]{1,0:T(8,128)(2,1)S(1)} fusion(bf16[128,3584]{1,0:T(8,128)(2,1)} %param.19, f32[128,3584]{1,0:T(8,128)S(1)} %get-tuple-element.20, f32[128]{0:T(128)S(1)} %get-tuple-element.22, f32[128]{0:T(128)S(1)} %get-tuple-element.19, f32[128]{0:T(128)S(1)} %get-tuple-element.18), kind=kLoop, calls=%fused_computation.10 | loop fusion | flops 2752512 | bytes 3671552 | tf_op jit(solution)/shard_map/convert_element_type | solution.py:564
  152.0 0.0 copy-start.6
  152.0 0.0 copy-start.7
  152.0 0.0 copy-start.9
  152.0 0.1 broadcast_select_fusion.1
  152.1 0.1 collective-permute-start
  152.2 1.0 copy-done.7
  153.2 0.1 convert_reduce_fusion
  154.6 0.2 fusion.22
  154.8 0.0 collective-permute-done
  154.8 6.1 %fusion.30 = (f32[128]{0:T(128)S(1)}, f32[128]{0:T(128)S(1)}, f32[128,1152]{1,0:T(8,128)S(1)}) fusion(f32[128]{0:T(128)S(1)} %add_rsqrt_fusion, f32[128]{0:T(128)S(1)} %broadcast_multiply_fusion.2, bf16[1,128,1152]{2,1,0:T(8,128)(2,1)S(1)} %copy-done.7, f32[1152]{0:T(1024)S(1)} %copy-done.9, bf16[1152,3584]{1,0:T(8,128)(2,1)} %param.27, ...), kind=kOutput, calls=%fused_computation.50 | convolution fusion | flops 1062125312 | bytes 10066433 | tf_op jit(solution)/shard_map/dot_general | solution.py:579
  161.0 1.0 fusion.26
  (15 shorter events, 0.1 us)
Async XLA Ops:
  97.1 1.6 copy-start.1
  98.7 1.0 copy-start.2
  99.7 1.0 copy-start.3
  100.8 0.7 copy-start.4
  101.5 0.7 copy-start.5
  112.8 1.3 copy-start
  114.2 23.5 %copy-start.10 = (s32[16]{0:T(128)S(1)}, s32[16]{0:T(128)}, u32[]{:S(2)}) copy-start(s32[16]{0:T(128)} %param.24) | copy-start | bytes 196
  114.2 24.1 %copy-start.8 = (f32[3584]{0:T(1024)S(1)}, f32[3584]{0:T(1024)}, u32[]{:S(2)}) copy-start(f32[3584]{0:T(1024)} %param.20) | copy-start | bytes 43012
  152.0 9.0 %copy-start.6 = (bf16[128,3584]{1,0:T(8,128)(2,1)}, bf16[128,3584]{1,0:T(8,128)(2,1)S(1)}, u32[]{:S(2)}) copy-start(bf16[128,3584]{1,0:T(8,128)(2,1)S(1)} %fusion.5) | copy-start | bytes 2752516
  152.0 1.2 copy-start.7
  152.0 2.8 %copy-start.9 = (f32[1152]{0:T(1024)S(1)}, f32[1152]{0:T(1024)}, u32[]{:S(2)}) copy-start(f32[1152]{0:T(1024)} %param.26) | copy-start | bytes 13828
  152.1 2.7 %collective-permute-start = (bf16[64,3584]{1,0:T(8,128)(2,1)S(1)}, bf16[64,3584]{1,0:T(8,128)(2,1)S(1)}, u32[]{:S(2)}, u32[]{:S(2)}) collective-permute-start(bf16[64,3584]{1,0:T(8,128)(2,1)S(1)} %get-tuple-element.15), channel_id=1, source_target_pairs={{0,2},{2,0},{4,6},{6,4},{8,10},{10,8},{12,14},{14,12},{16,18},{18,... | collective-permute-start | bytes 1376264 | tf_op jit(solution)/shard_map/ppermute | solution.py:522

commit v3 on v2

--- a/solution.py
+++ b/solution.py
@@ -22,17 +22,29 @@
 def attention_kernel(
     order_ref,
     mask_ref,
-    q_ref,
-    do_ref,
+    q_hbm,
+    do_hbm,
     delta_ref,
-    kv_ref,
+    kv_hbm,
     dq_ref,
     dkv_ref,
     slots,
     scores,
     dq_acc,
     acc,
+    q_ref,
+    do_ref,
+    kv_ref,
+    load_sem,
 ):
+    loads = [
+        pltpu.make_async_copy(source, target, load_sem.at[i])
+        for i, (source, target) in enumerate(
+            ((kv_hbm, kv_ref), (q_hbm, q_ref), (do_hbm, do_ref))
+        )
+    ]
+    for load in loads:
+        load.start()
     me = lax.axis_index("seq")
     blocks = order_ref.shape[0]
     half = q_ref.shape[0] // 2
@@ -46,6 +58,9 @@
     row = lax.broadcasted_iota(jnp.int32, (tall, lanes), 0)
     query_at = lax.rem(lax.broadcasted_iota(jnp.int32, (tall, lanes), 1), half)
     ahead = (row < half) & (row > query_at)
+
+    for load in loads:
+        load.wait()
 
     for b in range(2):
         own = 2 * me + b
@@ -158,26 +173,31 @@
     max_chunks = -(-blocks // CHUNK)
     smem = pl.BlockSpec(memory_space=pltpu.SMEM)
     vmem = pl.BlockSpec(memory_space=pltpu.VMEM)
+    anywhere = pl.BlockSpec(memory_space=pl.ANY)
     return pl.pallas_call(
         attention_kernel,
         out_shape=(
             jax.ShapeDtypeStruct((rows, HQ * HD), jnp.bfloat16),
             jax.ShapeDtypeStruct((keys, 2 * KVH * HD), jnp.bfloat16),
         ),
-        in_specs=[smem, smem, vmem, vmem, vmem, vmem],
+        in_specs=[smem, smem, anywhere, anywhere, vmem, anywhere],
         out_specs=(vmem, vmem),
         scratch_shapes=[
             pltpu.SMEM((blocks + CHUNK + 1,), jnp.int32),
             pltpu.VMEM((max_chunks, CHUNK * half, lanes), jnp.float32),
             pltpu.VMEM((HD, lanes), jnp.float32),
             pltpu.VMEM((keys, 2 * KVH * HD), jnp.float32),
+            pltpu.VMEM(queries.shape, queries.dtype),
+            pltpu.VMEM(out_grad.shape, out_grad.dtype),
+            pltpu.VMEM(kv.shape, kv.dtype),
+            pltpu.SemaphoreType.DMA((3,)),
         ],
         cost_estimate=pl.CostEstimate(
             flops=5 * rows * keys * HQ * HD,
             bytes_accessed=4 * keys * KVH * HD * 2 + 3 * rows * HQ * HD * 2,
             transcendentals=rows * keys * HQ // 2,
         ),
-        compiler_params=pltpu.CompilerParams(vmem_limit_bytes=48 * 1024 * 1024),
+        compiler_params=pltpu.CompilerParams(vmem_limit_bytes=67043328),
         name="attention_grads",
     )(order, mask, queries, out_grad, delta, kv)
 
@@ -212,10 +232,13 @@
 
 def gather_kernel(
     depth,
-    kv_ref,
+    k_ref,
+    v_ref,
     w_ref,
     kv_all,
     w_all,
+    kv_own,
+    w_own,
     own_sem,
     kv_recv,
     kv_core_recv,
@@ -226,22 +249,28 @@
     w_recv,
     w_x_recv,
     w_core_recv,
-    w_cx_recv,
     w_up,
     w_down,
     w_y,
     w_x,
     w_core,
-    w_cx,
 ):
     me, x, z, y, c = places()
     rows = w_ref.shape[0]
+    width = k_ref.shape[1]
     part = 5 * (rows // 16) // 14 * 16
     up, down = {"seq": me + 4}, {"seq": me - 4}
     beside, core = {"seq": me + 2 - 4 * y}, {"seq": me + 1 - 2 * c}
     across = {"batch": lax.axis_index("batch") + 1 - 2 * x}
     has_up, has_down = z < depth - 1, z > 0
 
+    loads = [
+        pltpu.make_async_copy(k_ref, kv_own.at[:, 0:width], own_sem.at[0]),
+        pltpu.make_async_copy(v_ref, kv_own.at[:, width : 2 * width], own_sem.at[1]),
+        pltpu.make_async_copy(w_ref, w_own, own_sem.at[2]),
+    ]
+    for load in loads:
+        load.start()
     barrier = pltpu.get_barrier_semaphore()
     for peer, present in (
         (up, has_up),
@@ -257,6 +286,8 @@
             ),
         )
     pl.semaphore_wait(barrier, 3 + has_up.astype(jnp.int32) + has_down.astype(jnp.int32))
+    for load in loads:
+        load.wait()
 
     started = []
 
@@ -272,18 +303,27 @@
             return [(z, None, None)]
         return [(z - step, z - step >= 0, True), (z + step, z + step < depth, False)]
 
+    def safe(j):
+        return jnp.clip(j, 0, depth - 1)
+
     def slot(j, side):
         return 2 * j + side
 
-    own_kv = pltpu.make_async_copy(kv_ref, kv_all.at[me], own_sem.at[0])
-    own_w = pltpu.make_async_copy(w_ref, w_all.at[me], own_sem.at[1])
+    def arrived(ref, semaphore, condition=None):
+        when(condition, remote(ref, ref, own_sem.at[3], semaphore, core).wait_recv)
+
+    own_kv = pltpu.make_async_copy(kv_own, kv_all.at[me], own_sem.at[4])
+    own_w = pltpu.make_async_copy(w_own, w_all.at[me], own_sem.at[5])
 
     def kv_at(u):
         return kv_all.at[2 * u + c]
 
-    def kv_pass(j, condition, upward, first):
+    def kv_core_pass(src, u, condition):
+        start(remote(src, kv_at(u), kv_core.at[u], kv_core_recv.at[u], core), condition)
+
+    def kv_pass(j, condition, upward):
         u = slot(j, y)
-        src = kv_ref if first else kv_at(u)
+        src = kv_own if upward is None else kv_at(u)
         if upward is not False:
             start(remote(src, kv_at(u), kv_up.at[j], kv_recv.at[u], up), both(condition, has_up))
         if upward is not True:
@@ -292,119 +332,128 @@
                 both(condition, has_down),
             )
         start(remote(src, kv_at(u), kv_y.at[j], kv_recv.at[u], beside), condition)
-        start(remote(src, kv_at(u), kv_core.at[u], kv_core_recv.at[u], core), condition)
-
-    def arrived(ref, semaphore, condition=None):
-        when(condition, remote(ref, ref, own_sem.at[2], semaphore, core).wait_recv)
-
-    def safe(j):
-        return jnp.clip(j, 0, depth - 1)
-
-    kv_pass(z, None, None, True)
+        kv_core_pass(src, u, condition)
+
+    spans = [
+        pl.ds(pl.multiple_of(x * (rows - part), 16), part),
+        pl.ds(part, rows - 2 * part),
+        pl.ds(pl.multiple_of((1 - x) * (rows - part), 16), part),
+    ]
+
+    def w_at(u, r):
+        return w_all.at[2 * u + c, spans[r]]
+
+    def w_core_pass(src, u, r, condition):
+        start(remote(src, w_at(u, r), w_core.at[r, u], w_core_recv.at[r, u], core), condition)
+
+    def w_share(u, r, condition):
+        if r == 0:
+            start(
+                remote(w_at(u, 0), w_at(u, 0), w_x.at[u], w_x_recv.at[u], across), condition
+            )
+        w_core_pass(w_at(u, r), u, r, condition)
+
+    def w_pass(j, r, condition, upward):
+        u = slot(j, y)
+        src = w_own.at[spans[r]] if upward is None else w_at(u, r)
+        dst = w_at(u, r)
+        if upward is not False:
+            start(remote(src, dst, w_up.at[r, j], w_recv.at[r, u], up), both(condition, has_up))
+        if upward is not True:
+            start(
+                remote(src, dst, w_down.at[r, j], w_recv.at[r, u], down),
+                both(condition, has_down),
+            )
+        start(remote(src, dst, w_y.at[r, j], w_recv.at[r, u], beside), condition)
+
+    kv_pass(z, None, None)
+    for r in (0, 1):
+        w_pass(z, r, None, None)
+    for r in (0, 1, 2):
+        w_core_pass(w_own.at[spans[r]], slot(z, y), r, None)
     own_kv.start()
     own_w.start()
-    for step in range(1, depth):
-        for j, condition, upward in line(step):
-            j = safe(j)
-            arrived(kv_at(slot(j, y)), kv_recv.at[slot(j, y)], condition)
-            kv_pass(j, condition, upward, False)
-
-    main = pl.ds(pl.multiple_of(x * part, 16), rows - part)
-    mine = pl.ds(pl.multiple_of(x * (rows - part), 16), part)
-    other = pl.ds(pl.multiple_of((1 - x) * (rows - part), 16), part)
-
-    def w_at(u, which):
-        return w_all.at[2 * u + c, which]
-
-    def w_pass(j, condition, upward, first):
-        u = slot(j, y)
-        src = w_ref.at[main] if first else w_at(u, main)
-        dst = w_at(u, main)
-        if upward is not False:
-            start(remote(src, dst, w_up.at[j], w_recv.at[u], up), both(condition, has_up))
-        if upward is not True:
-            start(remote(src, dst, w_down.at[j], w_recv.at[u], down), both(condition, has_down))
-        start(remote(src, dst, w_y.at[j], w_recv.at[u], beside), condition)
-
-    def w_share(u, condition):
-        start(
-            remote(w_at(u, mine), w_at(u, mine), w_x.at[u], w_x_recv.at[u], across), condition
-        )
-        start(
-            remote(w_at(u, main), w_at(u, main), w_core.at[u], w_core_recv.at[u], core), condition
-        )
-
-    def w_finish(u, condition):
-        arrived(w_at(u, other), w_x_recv.at[u], condition)
-        start(
-            remote(w_at(u, other), w_at(u, other), w_cx.at[u], w_cx_recv.at[u], core), condition
-        )
-
-    w_pass(z, None, None, True)
-    own_u = slot(z, y)
-    start(
-        remote(w_ref.at[main], w_at(own_u, main), w_core.at[own_u], w_core_recv.at[own_u], core)
-    )
-    start(remote(w_ref.at[other], w_at(own_u, other), w_cx.at[own_u], w_cx_recv.at[own_u], core))
-
-    for step in range(depth):
-        for j, condition, _ in line(step):
-            u = slot(safe(j), 1 - y)
-            arrived(kv_at(u), kv_recv.at[u], condition)
-            start(remote(kv_at(u), kv_at(u), kv_core.at[u], kv_core_recv.at[u], core), condition)
 
     waiting = []
     for step in range(1, depth + 1):
         shared = []
-        if step < depth:
-            for j, condition, upward in line(step):
-                j = safe(j)
+        ahead = [(safe(j), present, upward) for j, present, upward in line(step)]
+        ahead = ahead if step < depth else []
+        aside = [(slot(safe(j), 1 - y), present) for j, present, _ in line(step - 1)]
+        for j, condition, upward in ahead:
+            arrived(kv_at(slot(j, y)), kv_recv.at[slot(j, y)], condition)
+            kv_pass(j, condition, upward)
+        for u, condition in aside:
+            arrived(kv_at(u), kv_recv.at[u], condition)
+            kv_core_pass(kv_at(u), u, condition)
+        for r in (0, 1):
+            for j, condition, upward in ahead:
                 u = slot(j, y)
-                arrived(w_at(u, main), w_recv.at[u], condition)
-                w_pass(j, condition, upward, False)
-                w_share(u, condition)
-                shared.append((u, condition))
-        for j, condition, _ in line(step - 1):
-            u = slot(safe(j), 1 - y)
-            arrived(w_at(u, main), w_recv.at[u], condition)
-            w_share(u, condition)
-            shared.append((u, condition))
+                arrived(w_at(u, r), w_recv.at[r, u], condition)
+                w_pass(j, r, condition, upward)
+                w_share(u, r, condition)
+            for u, condition in aside:
+                arrived(w_at(u, r), w_recv.at[r, u], condition)
+                w_share(u, r, condition)
+        shared = [(slot(j, y), condition) for j, condition, _ in ahead] + aside
         for u, condition in waiting:
-            w_finish(u, condition)
+            arrived(w_at(u, 2), w_x_recv.at[u], condition)
+            w_core_pass(w_at(u, 2), u, 2, condition)
         waiting = shared
     for u, condition in waiting:
-        w_finish(u, condition)
+        arrived(w_at(u, 2), w_x_recv.at[u], condition)
+        w_core_pass(w_at(u, 2), u, 2, condition)
 
     for u in range(2 * depth):
         from_core = 2 * u + 1 - c
         arrived(kv_all.at[from_core], kv_core_recv.at[u])
-        arrived(w_all.at[from_core, main], w_core_recv.at[u])
-        arrived(w_all.at[from_core, other], w_cx_recv.at[u])
+        for r in (0, 1, 2):
+            arrived(w_all.at[from_core, spans[r]], w_core_recv.at[r, u])
     for condition, copy in started:
         when(condition, copy.wait_send)
     own_kv.wait()
     own_w.wait()
 
 
-def gather(kv, weight, count):
+def gather(keys, values, weight, count):
     depth = count // 4
-    line, pairs = pltpu.SemaphoreType.DMA((depth,)), pltpu.SemaphoreType.DMA((2 * depth,))
+    kv_shape = (keys.shape[0], 2 * keys.shape[1])
+
+    def sems(*shape):
+        return pltpu.SemaphoreType.DMA(shape)
+
+    pairs = 2 * depth
     anywhere = pl.BlockSpec(memory_space=pl.ANY)
-    vmem = pl.BlockSpec(memory_space=pltpu.VMEM)
     return pl.pallas_call(
         functools.partial(gather_kernel, depth),
         out_shape=(
-            jax.ShapeDtypeStruct((count,) + kv.shape, kv.dtype),
+            jax.ShapeDtypeStruct((count,) + kv_shape, keys.dtype),
             jax.ShapeDtypeStruct((count,) + weight.shape, weight.dtype),
         ),
-        in_specs=[vmem, vmem],
+        in_specs=[anywhere, anywhere, anywhere],
         out_specs=(anywhere, anywhere),
-        scratch_shapes=[pltpu.SemaphoreType.DMA((3,))]
-        + [pairs, pairs, line, line, line, pairs]
-        + [pairs, pairs, pairs, pairs, line, line, line, pairs, pairs, pairs],
+        scratch_shapes=[
+            pltpu.VMEM(kv_shape, keys.dtype),
+            pltpu.VMEM(weight.shape, weight.dtype),
+            sems(6),
+            sems(pairs),
+            sems(pairs),
+            sems(depth),
+            sems(depth),
+            sems(depth),
+            sems(pairs),
+            sems(2, pairs),
+            sems(pairs),
+            sems(3, pairs),
+            sems(2, depth),
+            sems(2, depth),
+            sems(2, depth),
+            sems(pairs),
+            sems(3, pairs),
+        ],
         compiler_params=pltpu.CompilerParams(collective_id=0, has_side_effects=True),
         name="gather",
-    )(kv, weight)
+    )(keys, values, weight)
 
 
 def reduce_kernel(
@@ -543,7 +592,7 @@
     my_index = lax.axis_index("seq")
     my_blocks = lax.dynamic_slice_in_dim(block_order, 2 * my_index, 2, 0)
     count = lax.axis_size("seq")
-    kv_all, weight_all = gather(jnp.concatenate([keys, values], axis=1), qkv_weight, count)
+    kv_all, weight_all = gather(keys, values, qkv_weight, count)
     kv = kv_all.reshape(count * tok_rows, kv_all.shape[2])
     weight = weight_all.reshape(count * qkv_weight.shape[0], qkv_weight.shape[1])
     query_grad, kv_part = attention_grads(

time: 163 us -> 149 us (0.914)
  Pallas kernels: 124 us -> 118 us
  local copies, waits for them, and re-layouts: 9.6 us -> 3.86 us
    pallas_call x1, Pallas kernels: 90.1 us -> 79.4 us  [gather(): pl.pallas_call(functools.partial(gather_kernel, depth), out_shape=(jax.Sh...]
    unnamed x22 -> x14, local copies, waits for them, and re-layouts: 7.35 us -> 1.04 us
    pallas_call x1, Pallas kernels: 10.7 us -> 14.8 us  [attention_grads(): pl.pallas_call(attention_kernel, out_shape=(jax.ShapeDtypeStruct((rows, H...]
where the time goes in v3:
time: 149 us
  Pallas kernels  118 us (79%)
  matrix products  17.4 us (12%)
  between operations  5.28 us (4%)
  local copies, waits for them, and re-layouts  3.86 us (3%)
  other arithmetic  3.68 us (2%)
    pallas_call x1, Pallas kernels, gather(): pl.pallas_call(functools.partial(gather_kernel, depth), out_shape=(jax.Sh...  79.4 us
    pallas_call x1, Pallas kernels, reduce_shards(): pl.pallas_call(functools.partial(reduce_kernel, depth), out_shape=jax.Sha...  24.1 us
    pallas_call x1, Pallas kernels, attention_grads(): pl.pallas_call(attention_kernel, out_shape=(jax.ShapeDtypeStruct((rows, H...  14.8 us
    dot_general x1, matrix products, body(): jnp.dot(head_grads, weight.T, preferred_element_type=jnp.float32)  11.2 us
    dot_general x1, matrix products, body(): jnp.dot(frame_rows, projector.T, preferred_element_type=jnp.float32)  6.14 us
  transfers between devices with their start and end apart: 1, of which 0 were waited for; matrix products, arithmetic and copies ran while one was open for 0% of the time, Pallas kernels for 0%

profile of v3, /device:TPU:0, one launch (start us, length us, event | category | flops | bytes accessed | tf_op | source)
XLA Modules:
  0.0 148.6 jit_solution(595536606614046357)
XLA Ops:
  0.6 0.7 dynamic_slice.3
  1.4 0.6 fusion.31
  4.5 0.8 reshape.65
  5.3 0.1 reshape.70
  5.4 0.6 pad.4.delta_ref
  6.0 79.4 %gather.1 = (bf16[16,128,512]{2,1,0:T(8,128)(2,1)}, bf16[16,224,2304]{2,1,0:T(8,128)(2,1)}) custom-call(bf16[128,256]{1,0:T(8,128)(2,1)} %k_ref.1, bf16[128,256]{1,0:T(8,128)(2,1)} %v_ref.1, bf16[224,2304]{1,0:T(8,128)(2,1)} %w_ref.1), custom_call_target="tpu_custom_call" | custom-call | tf_op jit(solution)/shard_map/gather/pallas_call | solution.py:427
  85.4 14.8 %attention_grads.1 = (bf16[128,1792]{1,0:T(8,128)(2,1)}, bf16[2048,512]{1,0:T(8,128)(2,1)}) custom-call(s32[32]{0:T(128)} %order_ref.1, s32[32,32]{1,0:T(8,128)} %mask_ref.1, bf16[128,1792]{1,0:T(8,128)(2,1)} %q_hbm.1, bf16[128,1792]{1,0:T(8,128)(2,1)} %do_hbm.1, f32[4,1,512]{2,1,0:T(1,128)} %pad.4.delta_ref, bf16[2048,512]{1,0:T(8,128)(2,1)} %bitcast.41), custom_call_target="tpu_custom_call" | custom-call | flops 2348810240 | bytes 5570560 | tf_op jit(solution)/shard_map/attention_grads/pallas_call | solution.py:177
  100.2 0.0 copy-start.6
  100.2 0.0 copy-start.1
  100.2 0.0 copy-start.3
  100.2 0.0 copy-start.4
  100.2 24.1 %reduce_shards.1 = bf16[128,512]{1,0:T(8,128)(2,1)} custom-call(bf16[16,128,512]{2,1,0:T(8,128)(2,1)} %bitcast.39), custom_call_target="tpu_custom_call" | custom-call | tf_op jit(solution)/shard_map/reduce_shards/pallas_call | solution.py:548
  124.4 0.0 copy-done.6
  124.4 0.6 fusion.27
  125.0 0.0 copy-done.1
  125.0 0.0 copy-done.3
  125.0 0.0 copy-done.4
  125.0 11.2 %fusion.2 = (f32[128]{0:T(128)S(1)}, f32[128]{0:T(128)S(1)}, f32[128,3584]{1,0:T(8,128)S(1)}) fusion(bf16[128,3584]{1,0:T(8,128)(2,1)S(1)} %copy-done.1, f32[3584]{0:T(1024)S(1)} %copy-done.4, bf16[3584,2304]{1,0:T(8,128)(2,1)} %bitcast.38, bf16[128,512]{1,0:T(8,128)(2,1)} %reduce_shards.1, bf16[128,1792]{1,0:T(8,128)(2,1)S(1)} %copy-done.3), kind=kOutput, calls=%fused_computation.7 | convolution fusion | flops 2118778624 | bytes 19872768 | tf_op jit(solution)/shard_map/dot_general | solution.py:603
  136.9 1.6 %fusion.5 = bf16[128,3584]{1,0:T(8,128)(2,1)S(1)} fusion(bf16[128,3584]{1,0:T(8,128)(2,1)} %param.19, f32[128,3584]{1,0:T(8,128)S(1)} %get-tuple-element.20, f32[128]{0:T(128)S(1)} %get-tuple-element.22, f32[128]{0:T(128)S(1)} %get-tuple-element.19, f32[128]{0:T(128)S(1)} %get-tuple-element.18), kind=kLoop, calls=%fused_computation.10 | loop fusion | flops 2752512 | bytes 3671552 | tf_op jit(solution)/shard_map/convert_element_type | solution.py:613
  138.6 0.0 copy-start
  138.6 0.0 copy-start.2
  138.6 0.0 copy-start.5
  138.6 0.1 broadcast_select_fusion.1
  138.7 0.1 collective-permute-start
  138.8 1.0 copy-done.2
  139.8 0.1 convert_reduce_fusion
  141.2 0.2 fusion.22
  141.4 0.0 collective-permute-done
  141.4 0.0 copy-done.5
  141.4 6.1 %fusion.30 = (f32[128]{0:T(128)S(1)}, f32[128]{0:T(128)S(1)}, f32[128,1152]{1,0:T(8,128)S(1)}) fusion(f32[128]{0:T(128)S(1)} %add_rsqrt_fusion, f32[128]{0:T(128)S(1)} %broadcast_multiply_fusion.2, bf16[1,128,1152]{2,1,0:T(8,128)(2,1)S(1)} %copy-done.2, f32[1152]{0:T(1024)S(1)} %copy-done.5, bf16[1152,3584]{1,0:T(8,128)(2,1)} %param.27, ...), kind=kOutput, calls=%fused_computation.49 | convolution fusion | flops 1062125312 | bytes 10066433 | tf_op jit(solution)/shard_map/dot_general | solution.py:628
  147.6 0.0 copy-done
  147.6 1.0 fusion.26
  (6 shorter events, 0.0 us)
Async XLA Ops:
  100.2 24.2 %copy-start.6 = (s32[16]{0:T(128)S(1)}, s32[16]{0:T(128)}, u32[]{:S(2)}) copy-start(s32[16]{0:T(128)} %param.24) | copy-start | bytes 196
  100.2 24.9 %copy-start.1 = (bf16[128,3584]{1,0:T(8,128)(2,1)S(1)}, bf16[128,3584]{1,0:T(8,128)(2,1)}, u32[]{:S(2)}) copy-start(bf16[128,3584]{1,0:T(8,128)(2,1)} %param.19) | copy-start | bytes 2752516
  100.2 24.9 %copy-start.3 = (bf16[128,1792]{1,0:T(8,128)(2,1)S(1)}, bf16[128,1792]{1,0:T(8,128)(2,1)}, u32[]{:S(2)}) copy-start(bf16[128,1792]{1,0:T(8,128)(2,1)} %get-tuple-element.7) | copy-start | bytes 1376260
  100.2 24.8 %copy-start.4 = (f32[3584]{0:T(1024)S(1)}, f32[3584]{0:T(1024)}, u32[]{:S(2)}) copy-start(f32[3584]{0:T(1024)} %param.20) | copy-start | bytes 43012
  138.6 9.0 %copy-start = (bf16[128,3584]{1,0:T(8,128)(2,1)}, bf16[128,3584]{1,0:T(8,128)(2,1)S(1)}, u32[]{:S(2)}) copy-start(bf16[128,3584]{1,0:T(8,128)(2,1)S(1)} %fusion.5) | copy-start | bytes 2752516
  138.6 1.2 copy-start.2
  138.6 2.8 %copy-start.5 = (f32[1152]{0:T(1024)S(1)}, f32[1152]{0:T(1024)}, u32[]{:S(2)}) copy-start(f32[1152]{0:T(1024)} %param.26) | copy-start | bytes 13828
  138.7 2.7 %collective-permute-start = (bf16[64,3584]{1,0:T(8,128)(2,1)S(1)}, bf16[64,3584]{1,0:T(8,128)(2,1)S(1)}, u32[]{:S(2)}, u32[]{:S(2)}) collective-permute-start(bf16[64,3584]{1,0:T(8,128)(2,1)S(1)} %get-tuple-element.15), channel_id=1, source_target_pairs={{0,2},{2,0},{4,6},{6,4},{8,10},{10,8},{12,14},{14,12},{16,18},{18,... | collective-permute-start | bytes 1376264 | tf_op jit(solution)/shard_map/ppermute | solution.py:571
